TPU v7x, 512 devices: a whole 4x4x16 slice. The times are simulated.
512 devices in a mesh: grp: 8 (over y_hi, x), sp: 64 (over y_lo, z, core).
Axes of the slice: x: 4, y: 4 (y_hi: 2, y_lo: 2; y = y_hi * 2 + y_lo), z: 16, core: 2. Of those that a mesh axis runs over, the one named last changes fastest.
Arguments:
- field: float32 [16, 128, 1024], P('grp', 'sp'), may hold values from -6 to 6
- mix_rate: float32 [128, 1024], P('sp'), may hold values from 0.05 to 2
- react: float32 [16, 16], replicated, may hold values from -1.5 to 1.5
- particles: float32 [16, 4194304], P(None, ('grp', 'sp')), may hold values from -6 to 6
- cells: int32 [2, 4194304], P(None, ('grp', 'sp')), may hold values from 0 to 2047
- counts: int32 [32768], P(('grp', 'sp')), may hold values from 1 to 128
- dest: int32 [32768], P(('grp', 'sp')), may hold values from 0 to 2, as said below
Outputs:
- field_out: float32 [16, 128, 1024], P('grp', 'sp')
- spread_out: float32 [16, 128, 1024], P('grp', 'sp')
- particles_out: float32 [16, 4194304], P(None, ('grp', 'sp'))
Inputs may be any that keep to these rules, and one draw needn't show every extreme that they name: cells[1] refers to the slab that the slot's block reaches after migration. Among each device's 64 blocks exactly 16 have dest 1 and exactly 16 have dest 2.
All inputs are finite; a program needn't handle non-finite values.
Results may differ from a plain program's by a relative error of at most 0.0055.
Values may be sent and summed in bfloat16 or wider, within the bound.
A program may use at most 64 MiB of HBM per device.

v0:
```python
import jax
import jax.numpy as jnp
from jax import lax
from jax.sharding import PartitionSpec as P

ROW_LENGTH = 32
MOVE = 16


NU_COEF = 0.15
KAPPA = 16.0
REACT_STEP = 0.5


def extended(block, sides, width):
    for axis, dim in sides:
        count = lax.axis_size(axis)
        forward = [(i, i + 1) for i in range(count - 1)]
        forward.append((count - 1, 0))
        backward = [(target, source) for source, target in forward]
        low = lax.ppermute(
            lax.slice_in_dim(block, block.shape[dim] - width, None, axis=dim), axis, forward
        )
        high = lax.ppermute(lax.slice_in_dim(block, 0, width, axis=dim), axis, backward)
        block = jnp.concatenate([low, block, high], axis=dim)
    return block


def sent_to_all(array, axis):
    copies = jnp.broadcast_to(array, (lax.axis_size(axis), *array.shape))
    return lax.all_to_all(copies, axis, split_axis=0, concat_axis=0, tiled=True)


def joined_along(tiles, dim):
    shape = list(tiles.shape[1:])
    shape[dim] *= tiles.shape[0]
    return jnp.moveaxis(tiles, 0, dim).reshape(shape)


def collect(array, axis, dim):
    tiles = sent_to_all(array, axis)
    return joined_along(tiles, dim)


def split_up(array, dim, devices):
    shape = array.shape
    tiles = array.reshape(*shape[:dim], devices, shape[dim] // devices, *shape[dim + 1 :])
    return jnp.moveaxis(tiles, dim, 0)


def sum_at_owner(array, axis, dim):
    tiles = split_up(array, dim, lax.axis_size(axis))
    arrived = lax.all_to_all(tiles, axis, split_axis=0, concat_axis=0, tiled=True)
    return arrived.astype(jnp.float32).sum(axis=0)


def taken_together(array, axis):
    everything = sent_to_all(array, axis)
    return jnp.sum(everything, axis=0)


def from_behind(value, axis, steps):
    count = lax.axis_size(axis)
    pairs = [(source, (source + steps) % count) for source in range(count)]
    return lax.ppermute(value, axis, pairs)


def diffuse(padded):
    field = padded[:, 1:-1]
    neighbour_slabs = padded[:, 2:] + padded[:, :-2]
    neighbour_slabs = neighbour_slabs + jnp.roll(field, 1, axis=2) + jnp.roll(field, -1, axis=2)
    neighbour_slabs = (
        neighbour_slabs + jnp.roll(field, ROW_LENGTH, axis=2) + jnp.roll(field, -ROW_LENGTH, axis=2)
    )
    return field + NU_COEF * (neighbour_slabs - 6.0 * field)


def diffuse_owned(field):
    padded = extended(field, (("sp", 1),), 1)
    return diffuse(padded)


def collect_owned_cells(diffused):
    return collect(diffused.astype(jnp.bfloat16), "grp", 0)


def combine_owned_sums(moments, width, cells_dev):
    sums = moments[: 2 * width].reshape(2, width, cells_dev)
    owned_sums = sum_at_owner(sums.astype(jnp.bfloat16), "grp", 1)
    total_count = taken_together(moments[2 * width], "grp")
    return (owned_sums, total_count)


def refresh(diffused, sums, count):
    return diffused + (sums[0] - count * diffused) / (count + KAPPA)


def spread_of(diffused, sums, count):
    return (sums[1] - 2.0 * diffused * sums[0] + count * diffused * diffused) / (count + KAPPA)


def live_mask(counts, total):
    blocks_dev = total // 128
    slot = lax.broadcasted_iota(jnp.int32, (blocks_dev, 128), 1)
    return (slot < counts[:, None]).astype(jnp.float32).reshape(total)


def weight_rows(rate_flat):
    weight = 1.0 - jnp.exp(-0.5 * rate_flat)
    upper_part = weight.astype(jnp.bfloat16)
    lower_part = (weight - upper_part.astype(jnp.float32)).astype(jnp.bfloat16)
    return jnp.stack([upper_part, lower_part], 0)


def advance(phi, cell_ids, live, shared_moments, extra_rows, react):
    width, total = phi.shape
    cells_dev = shared_moments.shape[1]
    table = jnp.concatenate([shared_moments, extra_rows], 0)
    span = min(1024, total)
    turns = total // span
    grid = lax.broadcasted_iota(jnp.int32, (cells_dev, 1), 0)

    def one_block(index, carry):
        result, moments = carry
        start = index * span
        piece = lax.dynamic_slice_in_dim(phi, start, span, 1)
        located = lax.dynamic_slice_in_dim(cell_ids, start, span, 0)
        alive = lax.dynamic_slice_in_dim(live, start, span, 0)
        onehot = (grid == located[None, :]).astype(jnp.bfloat16)
        looked = jnp.dot(table, onehot, preferred_element_type=jnp.float32)
        value = looked[:width]
        weight = looked[width] + looked[width + 1]
        mixed = piece + weight * (value - piece)
        stepped = mixed + REACT_STEP * jnp.tanh(
            jnp.dot(react.T, mixed, precision=lax.Precision.HIGHEST)
        )
        kept = alive * stepped
        rows = jnp.concatenate([kept, kept * stepped, alive[None]], 0).astype(jnp.bfloat16)
        deposit = lax.dot_general(
            rows, onehot, (((1,), (1,)), ((), ())), preferred_element_type=jnp.float32
        )
        return (lax.dynamic_update_slice_in_dim(result, stepped, start, 1), moments + deposit)

    initial = (jnp.zeros_like(phi), jnp.zeros((2 * width + 1, cells_dev), jnp.float32))
    return lax.fori_loop(0, turns, one_block, initial)


def migrate(phi, upcoming_cells, counts, dest):
    width, total = phi.shape
    blocks_dev = total // 128
    keep = blocks_dev - 2 * MOVE
    order = jnp.argsort(dest, stable=True)
    blocks = jnp.take(phi.reshape(width, blocks_dev, 128), order, axis=1)
    cell_blocks = jnp.take(upcoming_cells.reshape(blocks_dev, 128), order, axis=0).astype(
        jnp.float32
    )
    packed = jnp.concatenate([blocks, cell_blocks[None]], 0)
    block_sizes = jnp.take(counts, order).astype(jnp.float32)
    from_below = from_behind((packed[:, keep + MOVE :], block_sizes[keep + MOVE :]), "sp", 1)
    from_above = from_behind(
        (packed[:, keep : keep + MOVE], block_sizes[keep : keep + MOVE]), "sp", -1
    )
    merged = jnp.concatenate([packed[:, :keep], from_below[0], from_above[0]], 1)
    new_sizes = jnp.concatenate([block_sizes[:keep], from_below[1], from_above[1]], 0)
    moved = merged[:width].reshape(width, total)
    moved_cells = merged[width].reshape(total).astype(jnp.int32)
    return (moved, moved_cells, new_sizes.astype(jnp.int32))


def shards(field, mix_rate, react, particles, cells, counts, dest):
    owned, depth, plane = field.shape
    width, total = particles.shape
    cells_dev = depth * plane
    extra_rows = weight_rows(mix_rate.reshape(-1))
    live_first = live_mask(counts, total)
    diffused = diffuse_owned(field).reshape(owned, cells_dev)
    shared_moments = collect_owned_cells(diffused)
    stepped, moments = advance(particles, cells[0], live_first, shared_moments, extra_rows, react)
    moved, moved_cells, moved_counts = migrate(stepped, cells[1], counts, dest)
    live_next = live_mask(moved_counts, total)
    owned_sums, total_count = combine_owned_sums(moments, width, cells_dev)
    refreshed = refresh(diffused, owned_sums, total_count).reshape(owned, depth, plane)
    diffused = diffuse_owned(refreshed).reshape(owned, cells_dev)
    shared_moments = collect_owned_cells(diffused)
    final, moments = advance(moved, moved_cells, live_next, shared_moments, extra_rows, react)
    owned_sums, total_count = combine_owned_sums(moments, width, cells_dev)
    field_out = refresh(diffused, owned_sums, total_count).reshape(owned, depth, plane)
    spread_out = spread_of(diffused, owned_sums, total_count).reshape(owned, depth, plane)
    return (field_out, spread_out, live_next[None] * final)


def solution(mesh):
    return jax.shard_map(
        shards,
        mesh=mesh,
        in_specs=(
            P("grp", "sp", None),
            P("sp", None),
            P(),
            P(None, ("grp", "sp")),
            P(None, ("grp", "sp")),
            P(("grp", "sp")),
            P(("grp", "sp")),
        ),
        out_specs=(P("grp", "sp", None), P("grp", "sp", None), P(None, ("grp", "sp"))),
        check_vma=False,
    )
```

profile of v0, /device:TPU:2, one launch (start us, length us, event | category | flops | bytes accessed | tf_op | source)
XLA Modules:
  0.0 183.7 jit_solution(6103537896984729128)
XLA Ops:
  1.5 11.9 %collective-permute-start = (f32[2,1,1024]{2,1,0:T(1,128)S(1)}, f32[2,1,1024]{2,1,0:T(1,128)S(1)}, u32[]{:S(2)}, u32[]{:S(2)}) collective-permute-start(f32[2,1,1024]{2,1,0:T(1,128)S(1)} %get-tuple-element.443), channel_id=1, source_target_pairs={{1,0},{2,1},{3,2},{4,3},{5,4},{6,5},{7,6},{8,7},{9,8},{10,9},{11,1... | collective-permute-start | bytes 24584 | tf_op jit(solution)/shard_map/ppermute | solution.py:24
  13.4 1.9 %collective-permute-start.1 = (f32[2,1,1024]{2,1,0:T(1,128)S(1)}, f32[2,1,1024]{2,1,0:T(1,128)S(1)}, u32[]{:S(2)}, u32[]{:S(2)}) collective-permute-start(f32[2,1,1024]{2,1,0:T(1,128)S(1)} %get-tuple-element.444), channel_id=1, source_target_pairs={{0,1},{1,2},{2,3},{3,4},{4,5},{5,6},{6,7},{7,8},{8,9},{9,10},{10,1... | collective-permute-start | bytes 24584 | tf_op jit(solution)/shard_map/ppermute | solution.py:21
  15.3 2.7 %sort.17 = (s32[64]{0:T(128)}, s32[64]{0:T(128)S(1)}) sort(s32[64]{0:T(128)} %param.17, s32[64]{0:T(128)S(1)} %iota.30), dimensions={0}, to_apply=%region_4.5 | sort | flops 384 | bytes 1024 | tf_op jit(solution)/shard_map/jit(argsort)/sort | solution.py:152
  19.5 1.9 %collective-permute-start.6 = (f32[16]{0:T(128)S(1)}, f32[16]{0:T(128)S(1)}, u32[]{:S(2)}, u32[]{:S(2)}) collective-permute-start(f32[16]{0:T(128)S(1)} %get-tuple-element.453), channel_id=1, source_target_pairs={{0,1},{1,2},{2,3},{3,4},{4,5},{5,6},{6,7},{7,8},{8,9},{9,10},{10,1... | collective-permute-start | bytes 200 | tf_op jit(solution)/shard_map/ppermute | solution.py:65
  21.5 5.8 %collective-permute-start.7 = (f32[16]{0:T(128)S(1)}, f32[16]{0:T(128)S(1)}, u32[]{:S(2)}, u32[]{:S(2)}) collective-permute-start(f32[16]{0:T(128)S(1)} %get-tuple-element.454), channel_id=1, source_target_pairs={{0,63},{1,0},{2,1},{3,2},{4,3},{5,4},{6,5},{7,6},{8,7},{9,8},{10,9... | collective-permute-start | bytes 200 | tf_op jit(solution)/shard_map/ppermute | solution.py:65
  33.1 7.2 %all-to-all-start = ((bf16[8,2,2048]{2,1,0:T(2,128)(2,1)}), bf16[8,2,2048]{2,1,0:T(2,128)(2,1)S(1)}, u32[]{:S(2)}, u32[]{:S(2)}) async-start(bf16[8,2,2048]{2,1,0:T(2,128)(2,1)} %broadcast_in_dim.79), calls=%async_computation | async-start | bytes 131072 | tf_op jit(solution)/shard_map/all_to_all | solution.py:31
  40.4 6.5 %all-to-all-done = bf16[8,2,2048]{2,1,0:T(2,128)(2,1)S(1)} async-done(((bf16[8,2,2048]{2,1,0:T(2,128)(2,1)}), bf16[8,2,2048]{2,1,0:T(2,128)(2,1)S(1)}, u32[]{:S(2)}, u32[]{:S(2)}) %all-to-all-start) | async-done | bytes 65568 | tf_op jit(solution)/shard_map/all_to_all | solution.py:31
  47.0 34.8 %while.32 = (s32[]{:T(128)}, f32[16,8192]{1,0:T(8,128)S(1)}, f32[33,2048]{1,0:T(8,128)S(1)}, f32[16,8192]{1,0:T(8,128)}, s32[8192]{0:T(1024)S(1)}, /*index=5*/bf...) while((s32[]{:T(128)}, f32[16,8192]{1,0:T(8,128)S(1)}, ...), condition=%wide.region_1.2_spmd.clone, body=%wide.region_0.1_spmd.clone.sunk | while | flops 221786112 | bytes 1213621 | solution.py:145
  49.7 1.7 fusion.100
  54.0 1.7 fusion.100
  58.4 1.7 fusion.100
  62.7 1.7 fusion.100
  67.1 1.7 fusion.100
  71.4 1.7 fusion.100
  75.8 1.7 fusion.100
  80.1 1.7 fusion.100
  82.5 4.5 %all-to-all-start.2 = ((f32[8,1,2048]{2,1,0:T(1,128)}), f32[8,1,2048]{2,1,0:T(1,128)S(1)}, u32[]{:S(2)}, u32[]{:S(2)}) async-start(f32[8,1,2048]{2,1,0:T(1,128)} %broadcast_in_dim.80), calls=%async_computation.2 | async-start | bytes 131072 | tf_op jit(solution)/shard_map/all_to_all | solution.py:31
  88.8 1.9 %collective-permute-start.4 = (f32[17,16,128]{2,0,1:T(8,128)S(1)}, f32[17,16,128]{2,0,1:T(8,128)S(1)}, u32[]{:S(2)}, u32[]{:S(2)}) collective-permute-start(f32[17,16,128]{2,0,1:T(8,128)S(1)} %get-tuple-element.425), channel_id=1, source_target_pairs={{0,1},{1,2},{2,3},{3,4},{4,5},{5,6},{6,7},{7,8},{8,9},{9,10},{10,1... | collective-permute-start | bytes 417800 | tf_op jit(solution)/shard_map/ppermute | solution.py:65
  90.7 5.8 %collective-permute-start.5 = (f32[17,16,128]{2,0,1:T(8,128)S(1)}, f32[17,16,128]{2,0,1:T(8,128)S(1)}, u32[]{:S(2)}, u32[]{:S(2)}) collective-permute-start(f32[17,16,128]{2,0,1:T(8,128)S(1)} %get-tuple-element.426), channel_id=1, source_target_pairs={{0,63},{1,0},{2,1},{3,2},{4,3},{5,4},{6,5},{7,6},{8,7},{9,8},{10,9... | collective-permute-start | bytes 417800 | tf_op jit(solution)/shard_map/ppermute | solution.py:65
  96.5 7.3 %all-to-all-start.1 = ((bf16[8,2,2,2048]{3,2,1,0:T(2,128)(2,1)}), bf16[8,2,2,2048]{3,2,1,0:T(2,128)(2,1)S(1)}, u32[]{:S(2)}, u32[]{:S(2)}) async-start(bf16[8,2,2,2048]{3,2,1,0:T(2,128)(2,1)} %copy.22), calls=%async_computation.1 | async-start | bytes 262144 | tf_op jit(solution)/shard_map/all_to_all | solution.py:53
  103.8 6.8 %all-to-all-done.1 = bf16[8,2,2,2048]{3,2,1,0:T(2,128)(2,1)S(1)} async-done(((bf16[8,2,2,2048]{3,2,1,0:T(2,128)(2,1)}), bf16[8,2,2,2048]{3,2,1,0:T(2,128)(2,1)S(1)}, u32[]{:S(2)}, u32[]{:S(2)}) %all-to-all-start.1) | async-done | bytes 131104 | tf_op jit(solution)/shard_map/all_to_all | solution.py:53
  111.1 1.9 %collective-permute-start.2 = (f32[2,1,1024]{2,1,0:T(1,128)S(1)}, f32[2,1,1024]{2,1,0:T(1,128)S(1)}, u32[]{:S(2)}, u32[]{:S(2)}) collective-permute-start(f32[2,1,1024]{2,1,0:T(1,128)S(1)} %get-tuple-element.433), channel_id=1, source_target_pairs={{1,0},{2,1},{3,2},{4,3},{5,4},{6,5},{7,6},{8,7},{9,8},{10,9},{11,1... | collective-permute-start | bytes 24584 | tf_op jit(solution)/shard_map/ppermute | solution.py:24
  113.0 2.4 %collective-permute-start.3 = (f32[2,1,1024]{2,1,0:T(1,128)S(1)}, f32[2,1,1024]{2,1,0:T(1,128)S(1)}, u32[]{:S(2)}, u32[]{:S(2)}) collective-permute-start(f32[2,1,1024]{2,1,0:T(1,128)S(1)} %get-tuple-element.434), channel_id=1, source_target_pairs={{0,1},{1,2},{2,3},{3,4},{4,5},{5,6},{6,7},{7,8},{8,9},{9,10},{10,1... | collective-permute-start | bytes 24584 | tf_op jit(solution)/shard_map/ppermute | solution.py:21
  115.5 4.6 %collective-permute-done.3 = f32[2,1,1024]{2,1,0:T(1,128)S(1)} collective-permute-done((f32[2,1,1024]{2,1,0:T(1,128)S(1)}, f32[2,1,1024]{2,1,0:T(1,128)S(1)}, u32[]{:S(2)}, u32[]{:S(2)}) %collective-permute-start.3) | collective-permute-done | bytes 8224 | tf_op jit(solution)/shard_map/ppermute | solution.py:21
  120.9 4.4 %all-to-all-start.3 = ((bf16[8,2,2048]{2,1,0:T(2,128)(2,1)}), bf16[8,2,2048]{2,1,0:T(2,128)(2,1)S(1)}, u32[]{:S(2)}, u32[]{:S(2)}) async-start(bf16[8,2,2048]{2,1,0:T(2,128)(2,1)} %broadcast_in_dim.86), calls=%async_computation.3 | async-start | bytes 131072 | tf_op jit(solution)/shard_map/all_to_all | solution.py:31
  125.5 6.5 %all-to-all-done.3 = bf16[8,2,2048]{2,1,0:T(2,128)(2,1)S(1)} async-done(((bf16[8,2,2048]{2,1,0:T(2,128)(2,1)}), bf16[8,2,2048]{2,1,0:T(2,128)(2,1)S(1)}, u32[]{:S(2)}, u32[]{:S(2)}) %all-to-all-start.3) | async-done | bytes 65568 | tf_op jit(solution)/shard_map/all_to_all | solution.py:31
  132.1 27.5 %while.33 = (s32[]{:T(128)}, f32[16,8192]{1,0:T(8,128)S(1)}, f32[33,2048]{1,0:T(8,128)S(1)}, f32[16,8192]{1,0:T(8,128)S(1)}, s32[8192]{0:T(1024)S(1)}, /*index=5...) while((s32[]{:T(128)}, f32[16,8192]{1,0:T(8,128)S(1)}, ...), condition=%wide.region_6.7_spmd.clone, body=%wide.region_5.6_spmd.clone.sunk | while | flops 221786112 | bytes 1213621 | solution.py:145
  133.8 1.7 fusion.106
  160.2 4.5 %all-to-all-start.5 = ((f32[8,1,2048]{2,1,0:T(1,128)}), f32[8,1,2048]{2,1,0:T(1,128)S(1)}, u32[]{:S(2)}, u32[]{:S(2)}) async-start(f32[8,1,2048]{2,1,0:T(1,128)} %broadcast_in_dim.88), calls=%async_computation.5 | async-start | bytes 131072 | tf_op jit(solution)/shard_map/all_to_all | solution.py:31
  166.5 4.9 %all-to-all-done.5 = f32[8,1,2048]{2,1,0:T(1,128)S(1)} async-done(((f32[8,1,2048]{2,1,0:T(1,128)}), f32[8,1,2048]{2,1,0:T(1,128)S(1)}, u32[]{:S(2)}, u32[]{:S(2)}) %all-to-all-start.5) | async-done | bytes 65568 | tf_op jit(solution)/shard_map/all_to_all | solution.py:31
  171.4 4.6 %all-to-all-start.4 = ((bf16[8,2,2,2048]{3,2,1,0:T(2,128)(2,1)}), bf16[8,2,2,2048]{3,2,1,0:T(2,128)(2,1)S(1)}, u32[]{:S(2)}, u32[]{:S(2)}) async-start(bf16[8,2,2,2048]{3,2,1,0:T(2,128)(2,1)} %copy.26), calls=%async_computation.4 | async-start | bytes 262144 | tf_op jit(solution)/shard_map/all_to_all | solution.py:53
  176.0 6.9 %all-to-all-done.4 = bf16[8,2,2,2048]{3,2,1,0:T(2,128)(2,1)S(1)} async-done(((bf16[8,2,2,2048]{3,2,1,0:T(2,128)(2,1)}), bf16[8,2,2,2048]{3,2,1,0:T(2,128)(2,1)S(1)}, u32[]{:S(2)}, u32[]{:S(2)}) %all-to-all-start.4) | async-done | bytes 131104 | tf_op jit(solution)/shard_map/all_to_all | solution.py:53
  (193 shorter events, 61.8 us)
Async XLA Ops:
  0.6 31.7 %copy-start.2 = (f32[2,2,1024]{2,1,0:T(2,128)S(1)}, f32[2,2,1024]{2,1,0:T(2,128)}, u32[]{:S(2)}) copy-start(f32[2,2,1024]{2,1,0:T(2,128)} %param.11) | copy-start | bytes 49156
  0.6 30.7 %copy-start = (s32[64]{0:T(128)S(1)}, s32[64]{0:T(128)}, u32[]{:S(2)}) copy-start(s32[64]{0:T(128)} %param.16) | copy-start | bytes 772
  0.7 30.7 %copy-start.3 = (s32[2,8192]{1,0:T(2,128)S(1)}, s32[2,8192]{1,0:T(2,128)}, u32[]{:S(2)}) copy-start(s32[2,8192]{1,0:T(2,128)} %param.15) | copy-start | bytes 196612
  1.5 30.8 %collective-permute-start = (f32[2,1,1024]{2,1,0:T(1,128)S(1)}, f32[2,1,1024]{2,1,0:T(1,128)S(1)}, u32[]{:S(2)}, u32[]{:S(2)}) collective-permute-start(f32[2,1,1024]{2,1,0:T(1,128)S(1)} %get-tuple-element.443), channel_id=1, source_target_pairs={{1,0},{2,1},{3,2},{4,3},{5,4},{6,5},{7,6},{8,7},{9,8},{10,9},{11,1... | collective-permute-start | bytes 24584 | tf_op jit(solution)/shard_map/ppermute | solution.py:24
  13.4 18.9 %collective-permute-start.1 = (f32[2,1,1024]{2,1,0:T(1,128)S(1)}, f32[2,1,1024]{2,1,0:T(1,128)S(1)}, u32[]{:S(2)}, u32[]{:S(2)}) collective-permute-start(f32[2,1,1024]{2,1,0:T(1,128)S(1)} %get-tuple-element.444), channel_id=1, source_target_pairs={{0,1},{1,2},{2,3},{3,4},{4,5},{5,6},{6,7},{7,8},{8,9},{9,10},{10,1... | collective-permute-start | bytes 24584 | tf_op jit(solution)/shard_map/ppermute | solution.py:21
  19.5 12.7 %collective-permute-start.6 = (f32[16]{0:T(128)S(1)}, f32[16]{0:T(128)S(1)}, u32[]{:S(2)}, u32[]{:S(2)}) collective-permute-start(f32[16]{0:T(128)S(1)} %get-tuple-element.453), channel_id=1, source_target_pairs={{0,1},{1,2},{2,3},{3,4},{4,5},{5,6},{6,7},{7,8},{8,9},{9,10},{10,1... | collective-permute-start | bytes 200 | tf_op jit(solution)/shard_map/ppermute | solution.py:65
  21.5 10.8 %collective-permute-start.7 = (f32[16]{0:T(128)S(1)}, f32[16]{0:T(128)S(1)}, u32[]{:S(2)}, u32[]{:S(2)}) collective-permute-start(f32[16]{0:T(128)S(1)} %get-tuple-element.454), channel_id=1, source_target_pairs={{0,63},{1,0},{2,1},{3,2},{4,3},{5,4},{6,5},{7,6},{8,7},{9,8},{10,9... | collective-permute-start | bytes 200 | tf_op jit(solution)/shard_map/ppermute | solution.py:65
  31.4 15.5 %copy-start.1 = (f32[16,16]{1,0:T(8,128)S(1)}, f32[16,16]{1,0:T(8,128)}, u32[]{:S(2)}) copy-start(f32[16,16]{1,0:T(8,128)} %param.13) | copy-start | bytes 3076
  33.1 13.7 %all-to-all-start = ((bf16[8,2,2048]{2,1,0:T(2,128)(2,1)}), bf16[8,2,2048]{2,1,0:T(2,128)(2,1)S(1)}, u32[]{:S(2)}, u32[]{:S(2)}) async-start(bf16[8,2,2048]{2,1,0:T(2,128)(2,1)} %broadcast_in_dim.79), calls=%async_computation | async-start | bytes 131072 | tf_op jit(solution)/shard_map/all_to_all | solution.py:31
  82.5 14.0 %all-to-all-start.2 = ((f32[8,1,2048]{2,1,0:T(1,128)}), f32[8,1,2048]{2,1,0:T(1,128)S(1)}, u32[]{:S(2)}, u32[]{:S(2)}) async-start(f32[8,1,2048]{2,1,0:T(1,128)} %broadcast_in_dim.80), calls=%async_computation.2 | async-start | bytes 131072 | tf_op jit(solution)/shard_map/all_to_all | solution.py:31
  88.8 36.5 %collective-permute-start.4 = (f32[17,16,128]{2,0,1:T(8,128)S(1)}, f32[17,16,128]{2,0,1:T(8,128)S(1)}, u32[]{:S(2)}, u32[]{:S(2)}) collective-permute-start(f32[17,16,128]{2,0,1:T(8,128)S(1)} %get-tuple-element.425), channel_id=1, source_target_pairs={{0,1},{1,2},{2,3},{3,4},{4,5},{5,6},{6,7},{7,8},{8,9},{9,10},{10,1... | collective-permute-start | bytes 417800 | tf_op jit(solution)/shard_map/ppermute | solution.py:65
  90.7 34.6 %collective-permute-start.5 = (f32[17,16,128]{2,0,1:T(8,128)S(1)}, f32[17,16,128]{2,0,1:T(8,128)S(1)}, u32[]{:S(2)}, u32[]{:S(2)}) collective-permute-start(f32[17,16,128]{2,0,1:T(8,128)S(1)} %get-tuple-element.426), channel_id=1, source_target_pairs={{0,63},{1,0},{2,1},{3,2},{4,3},{5,4},{6,5},{7,6},{8,7},{9,8},{10,9... | collective-permute-start | bytes 417800 | tf_op jit(solution)/shard_map/ppermute | solution.py:65
  96.5 14.2 %all-to-all-start.1 = ((bf16[8,2,2,2048]{3,2,1,0:T(2,128)(2,1)}), bf16[8,2,2,2048]{3,2,1,0:T(2,128)(2,1)S(1)}, u32[]{:S(2)}, u32[]{:S(2)}) async-start(bf16[8,2,2,2048]{3,2,1,0:T(2,128)(2,1)} %copy.22), calls=%async_computation.1 | async-start | bytes 262144 | tf_op jit(solution)/shard_map/all_to_all | solution.py:53
  111.1 4.4 %collective-permute-start.2 = (f32[2,1,1024]{2,1,0:T(1,128)S(1)}, f32[2,1,1024]{2,1,0:T(1,128)S(1)}, u32[]{:S(2)}, u32[]{:S(2)}) collective-permute-start(f32[2,1,1024]{2,1,0:T(1,128)S(1)} %get-tuple-element.433), channel_id=1, source_target_pairs={{1,0},{2,1},{3,2},{4,3},{5,4},{6,5},{7,6},{8,7},{9,8},{10,9},{11,1... | collective-permute-start | bytes 24584 | tf_op jit(solution)/shard_map/ppermute | solution.py:24
  113.0 7.1 %collective-permute-start.3 = (f32[2,1,1024]{2,1,0:T(1,128)S(1)}, f32[2,1,1024]{2,1,0:T(1,128)S(1)}, u32[]{:S(2)}, u32[]{:S(2)}) collective-permute-start(f32[2,1,1024]{2,1,0:T(1,128)S(1)} %get-tuple-element.434), channel_id=1, source_target_pairs={{0,1},{1,2},{2,3},{3,4},{4,5},{5,6},{6,7},{7,8},{8,9},{9,10},{10,1... | collective-permute-start | bytes 24584 | tf_op jit(solution)/shard_map/ppermute | solution.py:21
  120.9 11.0 %all-to-all-start.3 = ((bf16[8,2,2048]{2,1,0:T(2,128)(2,1)}), bf16[8,2,2048]{2,1,0:T(2,128)(2,1)S(1)}, u32[]{:S(2)}, u32[]{:S(2)}) async-start(bf16[8,2,2048]{2,1,0:T(2,128)(2,1)} %broadcast_in_dim.86), calls=%async_computation.3 | async-start | bytes 131072 | tf_op jit(solution)/shard_map/all_to_all | solution.py:31
  160.2 11.1 %all-to-all-start.5 = ((f32[8,1,2048]{2,1,0:T(1,128)}), f32[8,1,2048]{2,1,0:T(1,128)S(1)}, u32[]{:S(2)}, u32[]{:S(2)}) async-start(f32[8,1,2048]{2,1,0:T(1,128)} %broadcast_in_dim.88), calls=%async_computation.5 | async-start | bytes 131072 | tf_op jit(solution)/shard_map/all_to_all | solution.py:31
  171.4 11.5 %all-to-all-start.4 = ((bf16[8,2,2,2048]{3,2,1,0:T(2,128)(2,1)}), bf16[8,2,2,2048]{3,2,1,0:T(2,128)(2,1)S(1)}, u32[]{:S(2)}, u32[]{:S(2)}) async-start(bf16[8,2,2,2048]{3,2,1,0:T(2,128)(2,1)} %copy.26), calls=%async_computation.4 | async-start | bytes 262144 | tf_op jit(solution)/shard_map/all_to_all | solution.py:53
where the time goes:
time: 185 us; the launch traced here: 184 us
  starting transfers between devices  65.9 us (36%)
  matrix products  60.6 us (33%)
  waiting for transfers between devices  36.1 us (20%)
  local copies, waits for them, and re-layouts  12.3 us (7%)
  other arithmetic  6.59 us (4%)
    dot_general x16, matrix products, one_block(): lax.dot_general(rows, onehot, (((1,), (1,)), ((), ())), preferred_element...  26.6 us
    dot_general x16, matrix products, one_block(): looked = jnp.dot(table, onehot, preferred_element_type=jnp.float32)  22.3 us
    all_to_all x4, starting transfers between devices, sent_to_all(): return lax.all_to_all(copies, axis, split_axis=0, concat_axis=0, tiled=True)  20.7 us
    all_to_all x4, waiting for transfers between devices, sent_to_all(): return lax.all_to_all(copies, axis, split_axis=0, concat_axis=0, tiled=True)  17.8 us
    ppermute x4, starting transfers between devices, from_behind(): return lax.ppermute(value, axis, pairs)  15.3 us
    ppermute x2, starting transfers between devices, extended(): lax.ppermute(lax.slice_in_dim(block, 0, width, axis=dim), axis, backward)  13.8 us
    all_to_all x2, waiting for transfers between devices, sum_at_owner(): lax.all_to_all(tiles, axis, split_axis=0, concat_axis=0, tiled=True)  13.7 us
    all_to_all x2, starting transfers between devices, sum_at_owner(): lax.all_to_all(tiles, axis, split_axis=0, concat_axis=0, tiled=True)  11.8 us
  transfers between devices with their start and end apart: 14, of which 6 were waited for; matrix products, arithmetic and copies ran while one was open for 8% of the time, Pallas kernels for 0%

commit v1 on v0

v1 whole, which is shorter than its diff:
```python
import functools

import jax
import jax.numpy as jnp
from jax import lax
from jax.experimental import pallas as pl
from jax.experimental.pallas import tpu as pltpu
from jax.sharding import PartitionSpec as P

NU_COEF = 0.15
KAPPA = 16.0
REACT_STEP = 0.5
ROW_LENGTH = 32
LANES = 128
LOW = 256
SUB = 512
BF = jnp.bfloat16
F32 = jnp.float32
MESH = pl.DeviceIdType.MESH


def lane_roll(x, shift):
    return pltpu.roll(x, shift % x.shape[1], 1)


def diffuse_rows(grid):
    rows = grid.shape[0]
    near = pltpu.roll(grid, 1, 0) + pltpu.roll(grid, rows - 1, 0)
    near = near + lane_roll(grid, 1) + lane_roll(grid, -1)
    near = near + lane_roll(grid, ROW_LENGTH) + lane_roll(grid, -ROW_LENGTH)
    return grid + NU_COEF * (near - 6.0 * grid)


def order_blocks(particles, cells, counts, dest, phi, cell0, cell1_row):
    blocks = phi.shape[1] // LANES
    move = blocks // 4
    lane = lax.broadcasted_iota(jnp.int32, (1, LANES), 1)

    def place(i, carry):
        c0, c1, c2 = carry
        d = dest[i]
        is0 = (d == 0).astype(jnp.int32)
        is1 = (d == 1).astype(jnp.int32)
        is2 = 1 - is0 - is1
        dst = pl.ds(pl.multiple_of((is0 * c0 + is1 * c1 + is2 * c2) * LANES, LANES), LANES)
        src = pl.ds(pl.multiple_of(i * LANES, LANES), LANES)
        alive = lane < counts[i]
        phi[:, dst] = particles[:, src]
        first = jnp.where(alive, cells[0:1, src], -1)
        cell0[:, dst] = jnp.broadcast_to(first, (8, LANES))
        cell1_row[:, dst] = jnp.where(alive, cells[1:2, src], -1)
        return c0 + is0, c1 + is1, c2 + is2

    start = (jnp.int32(0), jnp.int32(blocks - 2 * move), jnp.int32(blocks - move))
    lax.fori_loop(0, blocks, place, start, unroll=8)


def kernel(
    n_grp,
    n_sp,
    field,
    mix_rate,
    react,
    phi,
    cell0,
    cell1_row,
    field_out,
    spread_out,
    particles_out,
    moved,
    cell1,
    cell1_got,
    weight,
    onehot,
    grid,
    halo_send,
    halo_got,
    flat,
    table_got,
    table_f,
    table,
    own_bf,
    moment,
    sum_send0,
    sum_got0,
    sum_send1,
    sum_got1,
    count_f,
    count_got,
    mig_send,
    mig_got,
    halo_ssem,
    halo_rsem,
    cell_ssem,
    cell_rsem,
    mig_ssem,
    mig_rsem,
    ag_ssem,
    ag_rsem,
    cnt_ssem,
    cnt_rsem,
    rs_ssem,
    rs_rsem,
):
    own = field.shape[0]
    width, total = phi.shape
    blocks = total // LANES
    move = blocks // 4
    keep = blocks - 2 * move
    half = keep * LANES
    part = move * LANES
    tile = own * 8
    g = lax.axis_index("grp")
    s = lax.axis_index("sp")
    up = lax.rem(s + 1, n_sp)
    down = lax.rem(s + n_sp - 1, n_sp)

    def peer(d):
        return lax.rem(g + d, n_grp)

    def remote(src, dst, ssem, rsem, where):
        return pltpu.make_async_remote_copy(
            src_ref=src, dst_ref=dst, send_sem=ssem, recv_sem=rsem, device_id=where, device_id_type=MESH
        )

    pending = []

    def send(*args):
        copy = remote(*args)
        copy.start()
        pending.append(copy)
        return copy

    cb = (cell0, cell1)

    barrier = pltpu.get_barrier_semaphore()
    for where in [(g, up), (g, down)] + [(peer(d), s) for d in range(1, n_grp)]:
        pl.semaphore_signal(barrier, inc=1, device_id=where, device_id_type=MESH)

    for j in range(own):
        grid[4 * j + 1 : 4 * j + 2, :] = field[j, 0:1, :]
        grid[4 * j + 2 : 4 * j + 3, :] = field[j, 1:2, :]

    def stage_halo():
        for j in range(own):
            halo_send[0, j : j + 1, :] = grid[4 * j + 1 : 4 * j + 2, :]
            halo_send[1, j : j + 1, :] = grid[4 * j + 2 : 4 * j + 3, :]

    stage_halo()
    rate = mix_rate[...]
    full_weight = 1.0 - jnp.exp(-0.5 * rate)
    w_high = full_weight.astype(BF).astype(F32)
    w_low = full_weight - w_high
    for z in range(2):
        for q in range(4):
            h = 4 * z + q
            part_h = w_high[z : z + 1, q * LOW : (q + 1) * LOW]
            part_l = w_low[z : z + 1, q * LOW : (q + 1) * LOW]
            both = jnp.concatenate(
                [jnp.broadcast_to(part_h, (8, LOW)), jnp.broadcast_to(part_l, (8, LOW))], 0
            )
            table[h * width : (h + 1) * width, :] = both.astype(BF)

    pl.semaphore_wait(barrier, n_grp + 1)

    def send_halo(step):
        to_up = send(
            halo_send.at[1], halo_got.at[step, 0], halo_ssem.at[step, 0], halo_rsem.at[step, 0], (g, up)
        )
        to_down = send(
            halo_send.at[0], halo_got.at[step, 1], halo_ssem.at[step, 1], halo_rsem.at[step, 1], (g, down)
        )
        return [to_up, to_down]

    halos = send_halo(0)

    cell_copies = [
        send(
            cell1_row.at[:, pl.ds(half + part, part)],
            cell1_got.at[0],
            cell_ssem.at[0],
            cell_rsem.at[0],
            (g, up),
        ),
        send(
            cell1_row.at[:, pl.ds(half, part)], cell1_got.at[1], cell_ssem.at[1], cell_rsem.at[1], (g, down)
        ),
    ]

    def finish_halo(step):
        for copy in halos:
            copy.wait_recv()
        for j in range(own):
            grid[4 * j : 4 * j + 1, :] = halo_got[step, 0, j : j + 1, :]
            grid[4 * j + 3 : 4 * j + 4, :] = halo_got[step, 1, j : j + 1, :]

    def share(step):
        diffused = diffuse_rows(grid[...])
        for j in range(own):
            for z in range(2):
                for q in range(4):
                    row = j * 8 + z * 4 + q
                    flat[row : row + 1, :] = diffused[
                        4 * j + 1 + z : 4 * j + 2 + z, q * LOW : (q + 1) * LOW
                    ]
        shared = flat[...].astype(BF)
        own_bf[step] = shared
        mine = pl.ds(pl.multiple_of(g * tile, tile), tile)
        table_got[step, mine, :] = shared
        copies = []
        for d in range(1, n_grp):
            copies.append(
                send(
                    own_bf.at[step],
                    table_got.at[step, mine, :],
                    ag_ssem.at[step, d - 1],
                    ag_rsem.at[step, d - 1],
                    (peer(d), s),
                )
            )
        return diffused, copies

    def build_table(step):
        whole = table_got[step].astype(F32)
        table_f[0] = whole[:, :LANES]
        table_f[1] = whole[:, LANES:]
        for h in range(8):
            left = table_f[0, pl.ds(h, width, stride=8), :]
            right = table_f[1, pl.ds(h, width, stride=8), :]
            table[h * width : (h + 1) * width, :] = jnp.concatenate([left, right], 1).astype(BF)

    iota16 = lax.broadcasted_iota(jnp.int32, (16, SUB), 0).astype(F32).astype(BF)

    def build_onehot(step, start):
        cut = pl.ds(start, SUB)
        low = (cb[step][:, cut] & (LOW - 1)).astype(F32)
        gap = jnp.concatenate([low, low], 0).astype(BF) - iota16
        for t in range(LOW // 16):
            onehot[step, t * 16 : (t + 1) * 16, cut] = jnp.where(
                gap == jnp.asarray(16.0 * t, BF), jnp.asarray(1.0, BF), jnp.asarray(0.0, BF)
            )

    def look_up(step, start):
        cut = pl.ds(start, SUB)
        found = jnp.dot(table[...], onehot[step, :, cut], preferred_element_type=F32)
        cell = cb[step][:, cut]
        bits = []
        for b in range(3):
            bit = (cell & (LOW << b)) != 0
            bits.append(jnp.concatenate([bit, bit], 0) if width == 16 else bit)
        level = [found[h * width : (h + 1) * width] for h in range(8)]
        for bit in bits:
            level = [jnp.where(bit, level[i + 1], level[i]) for i in range(0, len(level), 2)]
        return level[0]

    def look_up_weight(step, start):
        both = look_up(step, start)
        weight[step, :, pl.ds(start, SUB)] = both[:8] + both[8:]

    def deposit_count(step):
        sums = jnp.zeros((16, LOW), F32)
        spot = lax.broadcasted_iota(jnp.int32, (8, SUB), 0)
        for start in range(0, total, SUB):
            cut = pl.ds(start, SUB)
            hit = jnp.where((cb[step][:, cut] >> 8) == spot, 1.0, 0.0)
            rows = jnp.concatenate([hit, jnp.zeros_like(hit)], 0).astype(BF)
            sums = sums + lax.dot_general(
                rows, onehot[step, :, cut], (((1,), (1,)), ((), ())), preferred_element_type=F32
            )
        count_f[step] = sums[:8]
        copies = []
        for d in range(1, n_grp):
            copies.append(
                send(
                    count_f.at[step],
                    count_got.at[step, d - 1],
                    cnt_ssem.at[step, d - 1],
                    cnt_rsem.at[step, d - 1],
                    (peer(d), s),
                )
            )
        return copies

    react_t = react[...].T
    r_high = react_t.astype(BF).astype(F32)
    r_low = react_t - r_high
    react3 = jnp.concatenate([r_high, r_high, r_low], 1).astype(BF)

    def advance(step, piece, start):
        cut = pl.ds(start, SUB)
        value = look_up(step, start)
        w8 = weight[step, :, cut]
        w16 = jnp.concatenate([w8, w8], 0)
        mixed = piece + w16 * (value - piece)
        high = mixed.astype(BF)
        low = (mixed - high.astype(F32)).astype(BF)
        stack = jnp.concatenate([high, low, high], 0)
        return mixed + REACT_STEP * jnp.tanh(jnp.dot(react3, stack, preferred_element_type=F32))

    def deposit(step, rows, start):
        cut = pl.ds(start, SUB)
        high = cb[step][:, cut] >> 8
        high = jnp.concatenate([high, high], 0)
        spread = jnp.concatenate(
            [jnp.where(high == h, r, 0.0) for r in rows for h in range(8)], 0
        ).astype(BF)
        return lax.dot_general(
            spread, onehot[step, :, cut], (((1,), (1,)), ((), ())), preferred_element_type=F32
        )

    def owner_rows(kind, owner):
        pieces = []
        for j in range(own):
            r = owner * own + j
            pieces.append(
                jnp.concatenate(
                    [moment[kind, 0, pl.ds(r, 8, stride=width), :], moment[kind, 1, pl.ds(r, 8, stride=width), :]],
                    1,
                )
            )
        return jnp.concatenate(pieces, 0).astype(BF)

    def set_moment(kind, sums):
        moment[kind, 0] = sums[:, :LANES]
        moment[kind, 1] = sums[:, LANES:]

    def to_grid(rows):
        for j in range(own):
            for z in range(2):
                for q in range(4):
                    row = j * 8 + z * 4 + q
                    grid[4 * j + 1 + z : 4 * j + 2 + z, q * LOW : (q + 1) * LOW] = rows[row : row + 1, :]
        return grid[...]

    def total_count(step, copies):
        for copy in copies:
            copy.wait_recv()
        sums = count_f[step]
        for d in range(n_grp - 1):
            sums = sums + count_got[step, d]
        return to_grid(jnp.concatenate([sums] * own, 0))

    for start in range(0, total, SUB):
        build_onehot(0, start)
    finish_halo(0)
    diffused, shares = share(0)
    for start in range(0, total, SUB):
        look_up_weight(0, start)
    count_copies0 = deposit_count(0)
    for copy in cell_copies:
        copy.wait_recv()
    cell1[:, :half] = jnp.broadcast_to(cell1_row[:, :half], (8, half))
    for side in range(2):
        cell1[:, pl.ds(half + side * part, part)] = jnp.broadcast_to(cell1_got[side], (8, part))
    for start in range(0, total, SUB):
        build_onehot(1, start)
    for start in range(0, total, SUB):
        look_up_weight(1, start)
    count_copies1 = deposit_count(1)
    for copy in shares:
        copy.wait_recv()
    build_table(0)

    sums = jnp.zeros((8 * width, LOW), F32)
    order_of = list(range(half, total, SUB)) + list(range(0, half, SUB))
    moves = []
    for start in order_of:
        stepped = advance(0, phi[:, start : start + SUB], start)
        if start < half:
            moved[:, start : start + SUB] = stepped
        else:
            side, at = (start - half) // part, (start - half) % part
            mig_send[side, :, at : at + SUB] = stepped.astype(BF)
            if at + SUB == part:
                where = (g, down) if side == 0 else (g, up)
                moves.append(
                    send(mig_send.at[side], mig_got.at[1 - side], mig_ssem.at[side], mig_rsem.at[1 - side], where)
                )
        sums = sums + deposit(0, [stepped], start)
    set_moment(0, sums)
    for owner in range(n_grp):
        sum_send0[owner] = owner_rows(0, owner)
    sum_copies = []
    for d in range(1, n_grp):
        sum_copies.append(
            send(sum_send0.at[peer(d)], sum_got0.at[d - 1], rs_ssem.at[0, d - 1], rs_rsem.at[0, d - 1], (peer(d), s))
        )
    count = total_count(0, count_copies0)
    first = sum_send0[g].astype(F32)
    for copy in sum_copies:
        copy.wait_recv()
    for d in range(n_grp - 1):
        first = first + sum_got0[d].astype(F32)
    first = to_grid(first)
    refreshed = diffused + (first - count * diffused) / (count + KAPPA)
    for copy in halos:
        copy.wait_send()
        pending.remove(copy)
    grid[...] = refreshed
    stage_halo()
    halos = send_halo(1)
    finish_halo(1)
    diffused, shares = share(1)
    count = total_count(1, count_copies1)
    for copy in shares:
        copy.wait_recv()
    build_table(1)
    for copy in moves:
        copy.wait_recv()

    sums = jnp.zeros((16 * width, LOW), F32)
    for start in range(0, total, SUB):
        cut = pl.ds(start, SUB)
        if start < half:
            piece = moved[:, cut]
        else:
            side, at = (start - half) // part, (start - half) % part
            piece = mig_got[side, :, at : at + SUB].astype(F32)
        stepped = advance(1, piece, start)
        dead = cell1[:, cut] < 0
        kept = jnp.where(jnp.concatenate([dead, dead], 0), 0.0, stepped)
        particles_out[:, cut] = kept
        sums = sums + deposit(1, [kept, kept * stepped], start)
    set_moment(0, sums[: 8 * width])
    set_moment(1, sums[8 * width :])
    for owner in range(n_grp):
        sum_send1[owner, 0] = owner_rows(0, owner)
        sum_send1[owner, 1] = owner_rows(1, owner)
    sum_copies = []
    for d in range(1, n_grp):
        sum_copies.append(
            send(sum_send1.at[peer(d)], sum_got1.at[d - 1], rs_ssem.at[1, d - 1], rs_rsem.at[1, d - 1], (peer(d), s))
        )
    first = sum_send1[g, 0].astype(F32)
    second = sum_send1[g, 1].astype(F32)
    for copy in sum_copies:
        copy.wait_recv()
    for d in range(n_grp - 1):
        first = first + sum_got1[d, 0].astype(F32)
        second = second + sum_got1[d, 1].astype(F32)
    first = to_grid(first)
    second = to_grid(second)
    refreshed = diffused + (first - count * diffused) / (count + KAPPA)
    spread = (second - 2.0 * diffused * first + count * diffused * diffused) / (count + KAPPA)
    for j in range(own):
        for z in range(2):
            row = 4 * j + 1 + z
            field_out[j, z : z + 1, :] = refreshed[row : row + 1, :]
            spread_out[j, z : z + 1, :] = spread[row : row + 1, :]
    for copy in pending:
        copy.wait_send()


def solution(mesh):
    n_grp, n_sp = mesh.shape["grp"], mesh.shape["sp"]

    def shards(field, mix_rate, react, particles, cells, counts, dest):
        own, depth, plane = field.shape
        width, total = particles.shape
        part = total // 4
        tile = own * 8
        vmem = pl.BlockSpec(memory_space=pltpu.VMEM)
        smem = pl.BlockSpec(memory_space=pltpu.SMEM)
        phi, cell0, cell1_row = pl.pallas_call(
            order_blocks,
            out_shape=(
                jax.ShapeDtypeStruct((width, total), F32),
                jax.ShapeDtypeStruct((8, total), jnp.int32),
                jax.ShapeDtypeStruct((1, total), jnp.int32),
            ),
            in_specs=[vmem, vmem, smem, smem],
            out_specs=(vmem, vmem, vmem),
            compiler_params=pltpu.CompilerParams(vmem_limit_bytes=4 * 1024 * 1024),
            name="order_blocks",
        )(particles, cells, counts, dest)
        others = n_grp - 1
        dma = pltpu.SemaphoreType.DMA
        return pl.pallas_call(
            functools.partial(kernel, n_grp, n_sp),
            out_shape=(
                jax.ShapeDtypeStruct(field.shape, F32),
                jax.ShapeDtypeStruct(field.shape, F32),
                jax.ShapeDtypeStruct(particles.shape, F32),
            ),
            in_specs=[vmem] * 6,
            out_specs=(vmem, vmem, vmem),
            scratch_shapes=[
                pltpu.VMEM((width, total // 2), F32),
                pltpu.VMEM((8, total), jnp.int32),
                pltpu.VMEM((2, 1, part), jnp.int32),
                pltpu.VMEM((2, 8, total), F32),
                pltpu.VMEM((2, LOW, total), BF),
                pltpu.VMEM((own * 4, plane), F32),
                pltpu.VMEM((2, own, plane), F32),
                pltpu.VMEM((2, 2, own, plane), F32),
                pltpu.VMEM((tile, LOW), F32),
                pltpu.VMEM((2, 8 * width, LOW), BF),
                pltpu.VMEM((2, 8 * width, LANES), F32),
                pltpu.VMEM((8 * width, LOW), BF),
                pltpu.VMEM((2, tile, LOW), BF),
                pltpu.VMEM((2, 2, 8 * width, LANES), F32),
                pltpu.VMEM((n_grp, tile, LOW), BF),
                pltpu.VMEM((others, tile, LOW), BF),
                pltpu.VMEM((n_grp, 2, tile, LOW), BF),
                pltpu.VMEM((others, 2, tile, LOW), BF),
                pltpu.VMEM((2, 8, LOW), F32),
                pltpu.VMEM((2, others, 8, LOW), F32),
                pltpu.VMEM((2, width, part), BF),
                pltpu.VMEM((2, width, part), BF),
                dma((2, 2)),
                dma((2, 2)),
                dma((2,)),
                dma((2,)),
                dma((2,)),
                dma((2,)),
                dma((2, others)),
                dma((2, others)),
                dma((2, others)),
                dma((2, others)),
                dma((2, others)),
                dma((2, others)),
            ],
            compiler_params=pltpu.CompilerParams(
                collective_id=0, has_side_effects=True, vmem_limit_bytes=48 * 1024 * 1024
            ),
            name="mixing",
        )(field, mix_rate, react, phi, cell0, cell1_row)

    return jax.shard_map(
        shards,
        mesh=mesh,
        in_specs=(
            P("grp", "sp", None),
            P("sp", None),
            P(),
            P(None, ("grp", "sp")),
            P(None, ("grp", "sp")),
            P(("grp", "sp")),
            P(("grp", "sp")),
        ),
        out_specs=(P("grp", "sp", None), P("grp", "sp", None), P(None, ("grp", "sp"))),
        check_vma=False,
    )
```

time: 185 us -> 54.9 us (0.30)
  the two profiles are of different devices: /device:TPU:2 before, /device:TPU:8 now
where the time goes in v1:
time: 54.9 us; the launch traced here: 54.7 us
  Pallas kernels  48.8 us (89%)
  local copies, waits for them, and re-layouts  5.2 us (9%)
  between operations  0.69 us (1%)
    pallas_call x1, Pallas kernels, shards(): pl.pallas_call(functools.partial(kernel, n_grp, n_sp), out_shape=(jax.Sha...  47.5 us
    unnamed x17, local copies, waits for them, and re-layouts  5.2 us
    pallas_call x1, Pallas kernels, shards(): pl.pallas_call(order_blocks, out_shape=(jax.ShapeDtypeStruct((width, tota...  1.32 us

profile of v1, /device:TPU:8, one launch (start us, length us, event | category | flops | bytes accessed | tf_op | source)
XLA Modules:
  0.0 54.7 jit_solution(11395254328830877026)
XLA Ops:
  0.6 0.0 copy-start
  0.6 1.0 %copy-done = f32[16,8192]{1,0:T(8,128)S(1)} copy-done((f32[16,8192]{1,0:T(8,128)S(1)}, f32[16,8192]{1,0:T(8,128)}, u32[]{:S(2)}) %copy-start) | copy-done | bytes 524312
  1.7 0.0 copy-start.1
  1.7 0.8 %copy-done.1 = s32[2,8192]{1,0:T(2,128)S(1)} copy-done((s32[2,8192]{1,0:T(2,128)S(1)}, s32[2,8192]{1,0:T(2,128)}, u32[]{:S(2)}) %copy-start.1) | copy-done | bytes 65560
  2.5 0.0 copy-start.5
  2.5 0.7 %copy-done.5 = s32[64]{0:T(128)S(1)} copy-done((s32[64]{0:T(128)S(1)}, s32[64]{0:T(128)}, u32[]{:S(2)}) %copy-start.5) | copy-done | bytes 280
  3.2 0.0 copy-start.6
  3.2 0.7 %copy-done.6 = s32[64]{0:T(128)S(1)} copy-done((s32[64]{0:T(128)S(1)}, s32[64]{0:T(128)}, u32[]{:S(2)}) %copy-start.6) | copy-done | bytes 280
  3.8 0.0 copy-start.2
  3.8 0.0 copy-start.3
  3.8 0.0 copy-start.4
  3.8 1.3 %order_blocks.1 = (f32[16,8192]{1,0:T(8,128)S(1)}, s32[8,8192]{1,0:T(8,128)S(1)}, s32[1,8192]{1,0:T(1,128)S(1)}) custom-call(f32[16,8192]{1,0:T(8,128)S(1)} %copy-done, s32[2,8192]{1,0:T(2,128)S(1)} %copy-done.1, s32[64]{0:T(128)S(1)} %copy-done.5, s32[64]{0:T(128)S(1)} %copy-done.6), custom_call_target="tpu_custom_call" | custom-call | tf_op jit(solution)/shard_map/order_blocks/pallas_call | solution.py:464
  5.2 0.0 copy-done.2
  5.2 0.0 copy-done.3
  5.2 0.0 copy-done.4
  5.2 47.5 %mixing.1 = (f32[2,2,1024]{2,1,0:T(2,128)S(1)}, f32[2,2,1024]{2,1,0:T(2,128)S(1)}, f32[16,8192]{1,0:T(8,128)S(1)}) custom-call(f32[2,2,1024]{2,1,0:T(2,128)S(1)} %copy-done.2, f32[2,1024]{1,0:T(2,128)S(1)} %copy-done.3, f32[16,16]{1,0:T(8,128)S(1)} %copy-done.4, f32[16,8192]{1,0:T(8,128)S(1)} %get-tuple-element.6.phi, s32[8,8192]{1,0:T(8,128)S(1)} %get-tuple-element.7.cell0, ...), custom_call_target="tpu_custom_call" | custom-call | tf_op jit(solution)/shard_map/mixing/pallas_call | solution.py:478
  52.7 0.6 %copy.13 = f32[2,2,1024]{2,1,0:T(2,128)} copy(f32[2,2,1024]{2,1,0:T(2,128)S(1)} %get-tuple-element.12) | data formatting | bytes 32768
  53.3 0.6 %copy.14 = f32[2,2,1024]{2,1,0:T(2,128)} copy(f32[2,2,1024]{2,1,0:T(2,128)S(1)} %get-tuple-element.13) | data formatting | bytes 32768
  53.9 0.8 %copy.15 = f32[16,8192]{1,0:T(8,128)} copy(f32[16,8192]{1,0:T(8,128)S(1)} %get-tuple-element.14) | data formatting | bytes 1048576
Async XLA Ops:
  0.6 1.0 %copy-start = (f32[16,8192]{1,0:T(8,128)S(1)}, f32[16,8192]{1,0:T(8,128)}, u32[]{:S(2)}) copy-start(f32[16,8192]{1,0:T(8,128)} %particles.1) | copy-start | bytes 1572868
  1.7 0.8 %copy-start.1 = (s32[2,8192]{1,0:T(2,128)S(1)}, s32[2,8192]{1,0:T(2,128)}, u32[]{:S(2)}) copy-start(s32[2,8192]{1,0:T(2,128)} %cells.1) | copy-start | bytes 196612
  2.5 0.7 %copy-start.5 = (s32[64]{0:T(128)S(1)}, s32[64]{0:T(128)}, u32[]{:S(2)}) copy-start(s32[64]{0:T(128)} %counts.1) | copy-start | bytes 772
  3.2 0.7 %copy-start.6 = (s32[64]{0:T(128)S(1)}, s32[64]{0:T(128)}, u32[]{:S(2)}) copy-start(s32[64]{0:T(128)} %dest.1) | copy-start | bytes 772
  3.8 1.3 %copy-start.2 = (f32[2,2,1024]{2,1,0:T(2,128)S(1)}, f32[2,2,1024]{2,1,0:T(2,128)}, u32[]{:S(2)}) copy-start(f32[2,2,1024]{2,1,0:T(2,128)} %field.1) | copy-start | bytes 49156
  3.8 1.3 %copy-start.3 = (f32[2,1024]{1,0:T(2,128)S(1)}, f32[2,1024]{1,0:T(2,128)}, u32[]{:S(2)}) copy-start(f32[2,1024]{1,0:T(2,128)} %mix_rate.1) | copy-start | bytes 24580
  3.8 1.4 %copy-start.4 = (f32[16,16]{1,0:T(8,128)S(1)}, f32[16,16]{1,0:T(8,128)}, u32[]{:S(2)}) copy-start(f32[16,16]{1,0:T(8,128)} %react.1) | copy-start | bytes 3076

commit v2 on v0

v2 whole, which is shorter than its diff:
```python
import functools

import jax
import jax.numpy as jnp
from jax import lax
from jax.experimental import pallas as pl
from jax.experimental.pallas import tpu as pltpu
from jax.sharding import PartitionSpec as P

NU_COEF = 0.15
KAPPA = 16.0
REACT_STEP = 0.5
ROW_LENGTH = 32
LANES = 128
TILES = 8
LOW = 256
SUB = 512
BF = jnp.bfloat16
F32 = jnp.float32
I32 = jnp.int32
MESH = pl.DeviceIdType.MESH
NT = (((1,), (1,)), ((), ()))


def plane_shift(rows, shift):
    count = rows.shape[0]
    lane = lax.broadcasted_iota(I32, (count, LANES), 1)
    turned = pltpu.roll(rows, shift % LANES, 1)
    step = 1 if shift > 0 else TILES - 1
    carried = pltpu.roll(turned.reshape(count // TILES, TILES, LANES), step, 1).reshape(count, LANES)
    return jnp.where(lane < shift, carried, turned) if shift > 0 else jnp.where(lane >= LANES + shift, carried, turned)


def diffuse(below, plane, above):
    near = below + above
    for shift in (1, -1, ROW_LENGTH, -ROW_LENGTH):
        near = near + plane_shift(plane, shift)
    return plane + NU_COEF * (near - 6.0 * plane)


def kernel(
    n_grp,
    n_sp,
    field_hbm,
    rate_hbm,
    react_hbm,
    particles,
    cells,
    counts_hbm,
    dest_hbm,
    field_out,
    spread_out,
    particles_out,
    field,
    rate,
    react,
    raw,
    raw_cells,
    counts,
    dest,
    cell_rows,
    low_rows,
    high_rows,
    cell1_send,
    cell1,
    phi,
    moved,
    high,
    weight,
    onehot,
    particles_new,
    field_new,
    spread_new,
    own_planes,
    plane_send,
    planes,
    turned,
    table,
    moment,
    sum_send0,
    sum_got0,
    sum_send1,
    sum_got1,
    count_own,
    count_got,
    mig_send,
    mig_got,
    local_sem,
    cell_ssem,
    cell_rsem,
    mig_ssem,
    mig_rsem,
    x_ssem,
    x_rsem,
    cnt_ssem,
    cnt_rsem,
    rs_ssem,
    rs_rsem,
):
    own = field.shape[0]
    width, total = particles.shape
    blocks = total // LANES
    move = blocks // 4
    keep = blocks - 2 * move
    half = keep * LANES
    part = move * LANES
    tile = own * TILES
    g = lax.axis_index("grp")
    s = lax.axis_index("sp")
    up = lax.rem(s + 1, n_sp)
    down = lax.rem(s + n_sp - 1, n_sp)
    mine = pl.ds(pl.multiple_of(g * tile, tile), tile)

    def peer(d):
        return lax.rem(g + d, n_grp)

    others = [(peer(d), s) for d in range(1, n_grp)]
    above = [(peer(d), up) for d in range(n_grp)]
    below = [(peer(d), down) for d in range(n_grp)]
    barrier = pltpu.get_barrier_semaphore()
    for where in others + above + below:
        pl.semaphore_signal(barrier, inc=1, device_id=where, device_id_type=MESH)

    pending = []

    def send(src, dst, ssem, rsem, where):
        copy = pltpu.make_async_remote_copy(
            src_ref=src, dst_ref=dst, send_sem=ssem, recv_sem=rsem, device_id=where, device_id_type=MESH
        )
        copy.start()
        pending.append(copy)
        return copy

    loads = [
        pltpu.make_async_copy(src, dst, local_sem.at[i])
        for i, (src, dst) in enumerate(
            [
                (field_hbm, field),
                (dest_hbm, dest),
                (counts_hbm, counts),
                (cells, raw_cells),
                (rate_hbm, rate),
                (react_hbm, react),
            ]
        )
    ]
    for load in loads:
        load.start()
    load_field, load_dest, load_counts, load_cells, load_rate, load_react = loads

    def load_block(i, _):
        src = particles.at[:, pl.ds(pl.multiple_of(i * LANES, LANES), LANES)]
        dst = raw.at[pl.ds(pl.multiple_of(i * width, width), width), :]
        pltpu.make_async_copy(src, dst, local_sem.at[6]).start()
        return 0

    lax.fori_loop(0, blocks, load_block, 0, unroll=8)

    def exchange(step, values):
        for z in range(2):
            rounded = values[z].astype(BF)
            plane_send[step, z] = rounded
            planes[step, 1 + z, mine, :] = rounded
        copies = []

        def one(src, dst, where):
            i = len(copies)
            copies.append(send(src, dst, x_ssem.at[step, i], x_rsem.at[step, i], where))

        for i in range(n_grp):
            one(plane_send.at[step, 1], planes.at[step, 0, mine, :], above[i])
            one(plane_send.at[step, 0], planes.at[step, 3, mine, :], below[i])
        for i in range(n_grp - 1):
            one(plane_send.at[step], planes.at[step, 1:3, mine, :], others[i])
        return copies

    load_field.wait()
    for j in range(own):
        for z in range(2):
            for t in range(TILES):
                own_planes[z, j * TILES + t : j * TILES + t + 1, :] = field[
                    j, z : z + 1, t * LANES : (t + 1) * LANES
                ]
    current = [own_planes[0], own_planes[1]]
    pl.semaphore_wait(barrier, 3 * n_grp - 1)
    copies = exchange(0, current)

    load_dest.wait()
    load_counts.wait()
    load_cells.wait()
    lane = lax.broadcasted_iota(I32, (1, LANES), 1)

    def place(i, carry):
        spot, c0, c1, c2 = carry
        d = dest[i]
        is0 = (d == 0).astype(I32)
        is1 = (d == 1).astype(I32)
        is2 = 1 - is0 - is1
        pos = is0 * c0 + is1 * c1 + is2 * c2
        alive = lane < counts[i]
        src = pl.ds(pl.multiple_of(i * LANES, LANES), LANES)
        cell_rows[0, pl.ds(i, 1), :] = jnp.where(alive, raw_cells[0:1, src], -1)
        cell_rows[1, pl.ds(i, 1), :] = jnp.where(alive, raw_cells[1:2, src], -1)
        spot = jnp.where((lane & (blocks - 1)) == i, pos, spot)
        return spot, c0 + is0, c1 + is1, c2 + is2

    spot, _, _, _ = lax.fori_loop(
        0, blocks, place, (jnp.zeros((1, LANES), I32), I32(0), I32(keep), I32(keep + move)), unroll=8
    )
    hit = lax.broadcasted_iota(I32, (blocks, LANES), 0) == spot
    swap = jnp.where(hit, 1.0, 0.0)
    reps = LANES // blocks
    swap = jnp.concatenate([swap, swap], 1).astype(BF)

    def in_order(parts):
        zero = jnp.zeros((2 * LANES - blocks * len(parts), parts[0].shape[1]), F32)
        return jnp.dot(swap, jnp.concatenate(parts + [zero], 0).astype(BF), preferred_element_type=F32)

    def split_cell(cell):
        tile_of = jnp.where(cell < 0, -1, (cell >> 7) & (TILES - 1))
        low = ((cell >> 10) & 1) * LANES + (cell & (LANES - 1))
        return tile_of.astype(F32), low.astype(F32)

    tile0, low0 = split_cell(cell_rows[0])
    tile1, low1 = split_cell(cell_rows[1])
    sorted_cells = in_order([jnp.concatenate([tile0, low0, tile1, low1], 1)])
    high_rows[...] = sorted_cells[:, :LANES]
    low_rows[...] = sorted_cells[:, LANES : 2 * LANES]
    cell1_send[...] = (sorted_cells[:, 2 * LANES : 3 * LANES] * LOW + sorted_cells[:, 3 * LANES :]).astype(I32)
    cell1[:keep, :] = cell1_send[:keep, :]
    cell_copies = [
        send(
            cell1_send.at[pl.ds(keep + move, move)],
            cell1.at[pl.ds(keep, move)],
            cell_ssem.at[0],
            cell_rsem.at[0],
            (g, up),
        ),
        send(
            cell1_send.at[pl.ds(keep, move)],
            cell1.at[pl.ds(keep + move, move)],
            cell_ssem.at[1],
            cell_rsem.at[1],
            (g, down),
        ),
    ]

    iota16 = lax.broadcasted_iota(I32, (16, SUB), 0).astype(F32).astype(BF)
    rows_of = SUB // LANES

    def cast_rows(ref, start, count):
        first = start // LANES
        return jnp.concatenate(
            [jnp.broadcast_to(ref[r : r + 1, :], (count, LANES)) for r in range(first, first + rows_of)], 1
        )

    def build_onehot(step, start):
        cut = pl.ds(start, SUB)
        gap = cast_rows(low_rows, start, 16).astype(BF) - iota16
        for t in range(LOW // 16):
            onehot[step, t * 16 : (t + 1) * 16, cut] = jnp.where(
                gap == jnp.asarray(16.0 * t, BF), jnp.asarray(1.0, BF), jnp.asarray(0.0, BF)
            )
        high[step, :, cut] = cast_rows(high_rows, start, 8).astype(I32)

    def look_up(step, start):
        cut = pl.ds(start, SUB)
        found = jnp.dot(table[...], onehot[step, :, cut], preferred_element_type=F32)
        at = high[step, :, cut]
        level = [found[h * width : (h + 1) * width] for h in range(TILES)]
        for b in range(3):
            bit = (at & (1 << b)) != 0
            bit = jnp.concatenate([bit, bit], 0)
            level = [jnp.where(bit, level[i + 1], level[i]) for i in range(0, len(level), 2)]
        return level[0]

    def look_up_weight(step, start):
        both = look_up(step, start)
        weight[step, :, pl.ds(start, SUB)] = both[:8] + both[8:]

    def deposit_count(step):
        sums = jnp.zeros((16, LOW), F32)
        row = lax.broadcasted_iota(I32, (TILES, SUB), 0)
        for start in range(0, total, SUB):
            cut = pl.ds(start, SUB)
            here = jnp.where(high[step, :, cut] == row, 1.0, 0.0)
            rows = jnp.concatenate([here, jnp.zeros_like(here)], 0).astype(BF)
            sums = sums + lax.dot_general(rows, onehot[step, :, cut], NT, preferred_element_type=F32)
        count_own[step] = sums[:TILES]
        return [
            send(
                count_own.at[step],
                count_got.at[step, i],
                cnt_ssem.at[step, i],
                cnt_rsem.at[step, i],
                others[i],
            )
            for i in range(n_grp - 1)
        ]

    def total_count(step, arrivals):
        for copy in arrivals:
            copy.wait_recv()
        sums = count_own[step]
        for i in range(n_grp - 1):
            sums = sums + count_got[step, i]
        return [jnp.concatenate([sums[:, z * LANES : (z + 1) * LANES]] * own, 0) for z in range(2)]

    def build_table(step):
        whole = [planes[step, i].astype(F32) for i in range(4)]
        for z in range(2):
            turned[z] = diffuse(whole[z], whole[z + 1], whole[z + 2])
        for z in range(2):
            for t in range(TILES):
                table[t * width : (t + 1) * width, z * LANES : (z + 1) * LANES] = turned[
                    z, pl.ds(t, width, stride=TILES), :
                ].astype(BF)

    def diffuse_own(step, values):
        low = planes[step, 0, mine, :].astype(F32)
        top = planes[step, 3, mine, :].astype(F32)
        return [diffuse(low, values[0], values[1]), diffuse(values[0], values[1], top)]

    load_rate.wait()
    full_weight = 1.0 - jnp.exp(-0.5 * rate[...])
    w_high = full_weight.astype(BF).astype(F32)
    w_low = full_weight - w_high
    for z in range(2):
        for t in range(TILES):
            cut = slice(t * LANES, (t + 1) * LANES)
            both = [jnp.broadcast_to(w[z : z + 1, cut], (8, LANES)) for w in (w_high, w_low)]
            table[t * width : (t + 1) * width, z * LANES : (z + 1) * LANES] = jnp.concatenate(both, 0).astype(BF)
    for start in range(0, total, SUB):
        build_onehot(0, start)
    arrivals0 = deposit_count(0)
    for start in range(0, total, SUB):
        look_up_weight(0, start)

    pltpu.make_async_copy(raw, raw, local_sem.at[6]).wait()
    for r in range(0, width, 2):
        parts = []
        rest = jnp.concatenate([raw[pl.ds(r + i, blocks, stride=width), :] for i in range(2)], 1)
        for _ in range(3):
            parts.append(rest.astype(BF).astype(F32))
            rest = rest - parts[-1]
        ordered = in_order(parts)
        for i in range(2):
            phi[pl.ds(r + i, blocks, stride=width), :] = ordered[:, i * LANES : (i + 1) * LANES]

    for copy in cell_copies:
        copy.wait_recv()
    cell = cell1[...]
    high_rows[...] = (cell >> 8).astype(F32)
    low_rows[...] = (cell & (LOW - 1)).astype(F32)
    for start in range(0, total, SUB):
        build_onehot(1, start)
    arrivals1 = deposit_count(1)
    for start in range(0, total, SUB):
        look_up_weight(1, start)

    load_react.wait()
    react_t = react[...].T
    r_high = react_t.astype(BF).astype(F32)
    r_low = react_t - r_high
    react3 = jnp.concatenate([r_high, r_high, r_low], 1).astype(BF)

    def advance(step, piece, start):
        cut = pl.ds(start, SUB)
        value = look_up(step, start)
        w8 = weight[step, :, cut]
        mixed = piece + jnp.concatenate([w8, w8], 0) * (value - piece)
        upper = mixed.astype(BF)
        lower = (mixed - upper.astype(F32)).astype(BF)
        stack = jnp.concatenate([upper, lower, upper], 0)
        return mixed + REACT_STEP * jnp.tanh(jnp.dot(react3, stack, preferred_element_type=F32))

    def deposit(step, rows, start):
        cut = pl.ds(start, SUB)
        at = high[step, :, cut]
        at = jnp.concatenate([at, at], 0)
        spread = jnp.concatenate([jnp.where(at == t, r, 0.0) for r in rows for t in range(TILES)], 0).astype(BF)
        return lax.dot_general(spread, onehot[step, :, cut], NT, preferred_element_type=F32)

    def set_moment(kind, sums):
        moment[kind, 0] = sums[:, :LANES]
        moment[kind, 1] = sums[:, LANES:]

    def owner_rows(kind, owner, z):
        return jnp.concatenate(
            [moment[kind, z, pl.ds(owner * own + j, TILES, stride=width), :] for j in range(own)], 0
        ).astype(BF)

    def refresh(values, first, count):
        return [d + (f - c * d) / (c + KAPPA) for d, f, c in zip(values, first, count)]

    for copy in copies:
        copy.wait_recv()
    build_table(0)
    sums = jnp.zeros((TILES * width, LOW), F32)
    moves = []
    for start in list(range(half, total, SUB)) + list(range(0, half, SUB)):
        first = start // LANES
        piece = jnp.concatenate([phi[r * width : (r + 1) * width, :] for r in range(first, first + rows_of)], 1)
        stepped = advance(0, piece, start)
        if start < half:
            moved[:, start : start + SUB] = stepped
        else:
            side, at = (start - half) // part, (start - half) % part
            mig_send[side, :, at : at + SUB] = stepped.astype(BF)
            if at + SUB == part:
                where = (g, down) if side == 0 else (g, up)
                moves.append(
                    send(mig_send.at[side], mig_got.at[1 - side], mig_ssem.at[side], mig_rsem.at[1 - side], where)
                )
        sums = sums + deposit(0, [stepped], start)
    set_moment(0, sums)
    for owner in range(n_grp):
        for z in range(2):
            sum_send0[owner, z] = owner_rows(0, owner, z)
    sum_copies = [
        send(sum_send0.at[others[i][0]], sum_got0.at[i], rs_ssem.at[0, i], rs_rsem.at[0, i], others[i])
        for i in range(n_grp - 1)
    ]
    diffused = diffuse_own(0, current)
    count = total_count(0, arrivals0)
    first = [sum_send0[g, z].astype(F32) for z in range(2)]
    for copy in sum_copies:
        copy.wait_recv()
    for i in range(n_grp - 1):
        first = [first[z] + sum_got0[i, z].astype(F32) for z in range(2)]
    current = refresh(diffused, first, count)
    copies = exchange(1, current)
    count = total_count(1, arrivals1)
    for copy in moves:
        copy.wait_recv()
    for copy in copies:
        copy.wait_recv()
    build_table(1)

    sums = jnp.zeros((2 * TILES * width, LOW), F32)
    for start in range(0, total, SUB):
        cut = pl.ds(start, SUB)
        if start < half:
            piece = moved[:, cut]
        else:
            side, at = (start - half) // part, (start - half) % part
            piece = mig_got[side, :, at : at + SUB].astype(F32)
        stepped = advance(1, piece, start)
        dead = high[1, :, cut] < 0
        kept = jnp.where(jnp.concatenate([dead, dead], 0), 0.0, stepped)
        particles_new[:, cut] = kept
        sums = sums + deposit(1, [kept, kept * stepped], start)
    store_particles = pltpu.make_async_copy(particles_new, particles_out, local_sem.at[0])
    store_particles.start()
    set_moment(0, sums[: TILES * width])
    set_moment(1, sums[TILES * width :])
    for owner in range(n_grp):
        for kind in range(2):
            for z in range(2):
                sum_send1[owner, kind, z] = owner_rows(kind, owner, z)
    sum_copies = [
        send(sum_send1.at[others[i][0]], sum_got1.at[i], rs_ssem.at[1, i], rs_rsem.at[1, i], others[i])
        for i in range(n_grp - 1)
    ]
    diffused = diffuse_own(1, current)
    first = [sum_send1[g, 0, z].astype(F32) for z in range(2)]
    second = [sum_send1[g, 1, z].astype(F32) for z in range(2)]
    for copy in sum_copies:
        copy.wait_recv()
    for i in range(n_grp - 1):
        first = [first[z] + sum_got1[i, 0, z].astype(F32) for z in range(2)]
        second = [second[z] + sum_got1[i, 1, z].astype(F32) for z in range(2)]
    refreshed = refresh(diffused, first, count)
    for z in range(2):
        d, c = diffused[z], count[z]
        spread = (second[z] - 2.0 * d * first[z] + c * d * d) / (c + KAPPA)
        for j in range(own):
            for t in range(TILES):
                row, cut = j * TILES + t, slice(t * LANES, (t + 1) * LANES)
                field_new[j, z : z + 1, cut] = refreshed[z][row : row + 1, :]
                spread_new[j, z : z + 1, cut] = spread[row : row + 1, :]
    store_field = pltpu.make_async_copy(field_new, field_out, local_sem.at[1])
    store_spread = pltpu.make_async_copy(spread_new, spread_out, local_sem.at[2])
    store_field.start()
    store_spread.start()
    for copy in pending:
        copy.wait_send()
    for copy in (store_particles, store_field, store_spread):
        copy.wait()


def put_out(particles, field, spread, particles_out, field_out, spread_out, *scratch):
    buffers, sem = scratch[:-1], scratch[-1]
    ways = []
    for i, (src, dst) in enumerate([(particles, particles_out), (field, field_out), (spread, spread_out)]):
        take = pltpu.make_async_copy(src, buffers[i], sem.at[i])
        put = pltpu.make_async_copy(buffers[i], dst, sem.at[i])
        ways.append((take, put))
    for take, _ in ways:
        take.start()
    for take, put in ways:
        take.wait()
        put.start()
    for _, put in ways:
        put.wait()


def solution(mesh):
    n_grp, n_sp = mesh.shape["grp"], mesh.shape["sp"]

    def shards(field, mix_rate, react, particles, cells, counts, dest):
        own, depth, plane = field.shape
        width, total = particles.shape
        blocks = total // LANES
        part = total // 4
        tile = own * TILES
        rows = width * TILES
        hbm = pl.BlockSpec(memory_space=pltpu.HBM)
        others = n_grp - 1
        spread = 3 * n_grp - 1
        dma = pltpu.SemaphoreType.DMA
        shapes = (
            jax.ShapeDtypeStruct(field.shape, F32),
            jax.ShapeDtypeStruct(field.shape, F32),
            jax.ShapeDtypeStruct(particles.shape, F32),
        )
        results = pl.pallas_call(
            functools.partial(kernel, n_grp, n_sp),
            out_shape=shapes,
            in_specs=[hbm] * 7,
            out_specs=(hbm, hbm, hbm),
            scratch_shapes=[
                pltpu.VMEM(field.shape, F32),
                pltpu.VMEM(mix_rate.shape, F32),
                pltpu.VMEM(react.shape, F32),
                pltpu.VMEM((blocks * width, LANES), F32),
                pltpu.VMEM((2, total), I32),
                pltpu.SMEM((blocks,), I32),
                pltpu.SMEM((blocks,), I32),
                pltpu.VMEM((2, blocks, LANES), I32),
                pltpu.VMEM((blocks, LANES), F32),
                pltpu.VMEM((blocks, LANES), F32),
                pltpu.VMEM((blocks, LANES), I32),
                pltpu.VMEM((blocks, LANES), I32),
                pltpu.VMEM((blocks * width, LANES), F32),
                pltpu.VMEM((width, total // 2), F32),
                pltpu.VMEM((2, TILES, total), I32),
                pltpu.VMEM((2, 8, total), F32),
                pltpu.VMEM((2, LOW, total), BF),
                pltpu.VMEM(particles.shape, F32),
                pltpu.VMEM(field.shape, F32),
                pltpu.VMEM(field.shape, F32),
                pltpu.VMEM((2, tile, LANES), F32),
                pltpu.VMEM((2, 2, tile, LANES), BF),
                pltpu.VMEM((2, 4, rows, LANES), BF),
                pltpu.VMEM((2, rows, LANES), F32),
                pltpu.VMEM((rows, LOW), BF),
                pltpu.VMEM((2, 2, rows, LANES), F32),
                pltpu.VMEM((n_grp, 2, tile, LANES), BF),
                pltpu.VMEM((others, 2, tile, LANES), BF),
                pltpu.VMEM((n_grp, 2, 2, tile, LANES), BF),
                pltpu.VMEM((others, 2, 2, tile, LANES), BF),
                pltpu.VMEM((2, TILES, LOW), F32),
                pltpu.VMEM((2, others, TILES, LOW), F32),
                pltpu.VMEM((2, width, part), BF),
                pltpu.VMEM((2, width, part), BF),
                dma((7,)),
                dma((2,)),
                dma((2,)),
                dma((2,)),
                dma((2,)),
                dma((2, spread)),
                dma((2, spread)),
                dma((2, others)),
                dma((2, others)),
                dma((2, others)),
                dma((2, others)),
            ],
            compiler_params=pltpu.CompilerParams(
                collective_id=0, has_side_effects=True, vmem_limit_bytes=67043328
            ),
            name="mixing",
        )(field, mix_rate, react, particles, cells, counts, dest)
        field_new, spread_new, particles_new = results
        particles_new, field_new, spread_new = pl.pallas_call(
            put_out,
            out_shape=(shapes[2], shapes[0], shapes[1]),
            in_specs=[hbm] * 3,
            out_specs=(hbm, hbm, hbm),
            scratch_shapes=[
                pltpu.VMEM(particles.shape, F32),
                pltpu.VMEM(field.shape, F32),
                pltpu.VMEM(field.shape, F32),
                dma((3,)),
            ],
            compiler_params=pltpu.CompilerParams(vmem_limit_bytes=67043328),
            name="put_out",
        )(particles_new, field_new, spread_new)
        return field_new, spread_new, particles_new

    return jax.shard_map(
        shards,
        mesh=mesh,
        in_specs=(
            P("grp", "sp", None),
            P("sp", None),
            P(),
            P(None, ("grp", "sp")),
            P(None, ("grp", "sp")),
            P(("grp", "sp")),
            P(("grp", "sp")),
        ),
        out_specs=(P("grp", "sp", None), P("grp", "sp", None), P(None, ("grp", "sp"))),
        check_vma=False,
    )
```

time: 185 us -> 49.1 us (0.27)
  the two profiles are of different devices: /device:TPU:2 before, /device:TPU:1 now
where the time goes in v2:
time: 49.1 us; the launch traced here: 49 us
  Pallas kernels  48.3 us (98%)
  between operations  0.64 us (1%)
    pallas_call x1, Pallas kernels, shards(): pl.pallas_call(functools.partial(kernel, n_grp, n_sp), out_shape=shapes,...  46.5 us
    pallas_call x1, Pallas kernels, shards(): pl.pallas_call(put_out, out_shape=(shapes[2], shapes[0], shapes[1]), in_s...  1.86 us

profile of v2, /device:TPU:1, one launch (start us, length us, event | category | flops | bytes accessed | tf_op | source)
XLA Modules:
  0.0 49.0 jit_solution(3647987231726223846)
XLA Ops:
  0.6 46.5 %mixing.1 = (f32[2,2,1024]{2,1,0:T(2,128)}, f32[2,2,1024]{2,1,0:T(2,128)}, f32[16,8192]{1,0:T(8,128)}) custom-call(f32[2,2,1024]{2,1,0:T(2,128)} %field_hbm.1, f32[2,1024]{1,0:T(2,128)} %rate_hbm.1, f32[16,16]{1,0:T(8,128)} %react_hbm.1, f32[16,8192]{1,0:T(8,128)} %particles.1, s32[2,8192]{1,0:T(2,128)} %cells.1, s32[64]{0:T(128)} %counts_hbm.1, s32[64]{0:T(128)} %dest_hbm.1), custom_call_target="tpu_custom_call" | custom-call | tf_op jit(solution)/shard_map/mixing/pallas_call | solution.py:527
  47.1 1.9 %put_out.1 = (f32[16,8192]{1,0:T(8,128)}, f32[2,2,1024]{2,1,0:T(2,128)}, f32[2,2,1024]{2,1,0:T(2,128)}) custom-call(f32[16,8192]{1,0:T(8,128)} %get-tuple-element.9.particles, f32[2,2,1024]{2,1,0:T(2,128)} %get-tuple-element.10.field, f32[2,2,1024]{2,1,0:T(2,128)} %get-tuple-element.11.spread), custom_call_target="tpu_custom_call" | custom-call | tf_op jit(solution)/shard_map/put_out/pallas_call | solution.py:585

commit v3 on v2

--- a/solution.py
+++ b/solution.py
@@ -14,7 +14,7 @@
 LANES = 128
 TILES = 8
 LOW = 256
-SUB = 512
+SUB = 2048
 BF = jnp.bfloat16
 F32 = jnp.float32
 I32 = jnp.int32
@@ -76,6 +76,7 @@
     planes,
     turned,
     table,
+    weight_table,
     moment,
     sum_send0,
     sum_got0,
@@ -248,24 +249,30 @@
     iota16 = lax.broadcasted_iota(I32, (16, SUB), 0).astype(F32).astype(BF)
     rows_of = SUB // LANES
 
-    def cast_rows(ref, start, count):
-        first = start // LANES
+    def loop(start, stop, body, unroll=1):
+        def turn(i, _):
+            body(i, pl.multiple_of(i * SUB, SUB))
+            return 0
+
+        lax.fori_loop(start // SUB, stop // SUB, turn, 0, unroll=unroll)
+
+    def cast_rows(ref, index, count):
         return jnp.concatenate(
-            [jnp.broadcast_to(ref[r : r + 1, :], (count, LANES)) for r in range(first, first + rows_of)], 1
+            [jnp.broadcast_to(ref[pl.ds(index * rows_of + r, 1), :], (count, LANES)) for r in range(rows_of)], 1
         )
 
-    def build_onehot(step, start):
+    def build_onehot(step, index, start):
         cut = pl.ds(start, SUB)
-        gap = cast_rows(low_rows, start, 16).astype(BF) - iota16
+        gap = cast_rows(low_rows, index, 16).astype(BF) - iota16
         for t in range(LOW // 16):
             onehot[step, t * 16 : (t + 1) * 16, cut] = jnp.where(
                 gap == jnp.asarray(16.0 * t, BF), jnp.asarray(1.0, BF), jnp.asarray(0.0, BF)
             )
-        high[step, :, cut] = cast_rows(high_rows, start, 8).astype(I32)
-
-    def look_up(step, start):
+        high[step, :, cut] = cast_rows(high_rows, index, 8).astype(I32)
+
+    def look_up(step, start, rows):
         cut = pl.ds(start, SUB)
-        found = jnp.dot(table[...], onehot[step, :, cut], preferred_element_type=F32)
+        found = jnp.dot(rows[...], onehot[step, :, cut], preferred_element_type=F32)
         at = high[step, :, cut]
         level = [found[h * width : (h + 1) * width] for h in range(TILES)]
         for b in range(3):
@@ -274,19 +281,20 @@
             level = [jnp.where(bit, level[i + 1], level[i]) for i in range(0, len(level), 2)]
         return level[0]
 
-    def look_up_weight(step, start):
-        both = look_up(step, start)
-        weight[step, :, pl.ds(start, SUB)] = both[:8] + both[8:]
-
-    def deposit_count(step):
-        sums = jnp.zeros((16, LOW), F32)
+    def weigh(step):
         row = lax.broadcasted_iota(I32, (TILES, SUB), 0)
-        for start in range(0, total, SUB):
+        count_own[step] = jnp.zeros((TILES, LOW), F32)
+
+        def add(_, start):
             cut = pl.ds(start, SUB)
             here = jnp.where(high[step, :, cut] == row, 1.0, 0.0)
             rows = jnp.concatenate([here, jnp.zeros_like(here)], 0).astype(BF)
-            sums = sums + lax.dot_general(rows, onehot[step, :, cut], NT, preferred_element_type=F32)
-        count_own[step] = sums[:TILES]
+            sums = lax.dot_general(rows, onehot[step, :, cut], NT, preferred_element_type=F32)
+            count_own[step] = count_own[step] + sums[:TILES]
+            both = look_up(step, start, weight_table)
+            weight[step, :, cut] = both[:8] + both[8:]
+
+        loop(0, total, add, 1)
         return [
             send(
                 count_own.at[step],
@@ -329,12 +337,9 @@
         for t in range(TILES):
             cut = slice(t * LANES, (t + 1) * LANES)
             both = [jnp.broadcast_to(w[z : z + 1, cut], (8, LANES)) for w in (w_high, w_low)]
-            table[t * width : (t + 1) * width, z * LANES : (z + 1) * LANES] = jnp.concatenate(both, 0).astype(BF)
-    for start in range(0, total, SUB):
-        build_onehot(0, start)
-    arrivals0 = deposit_count(0)
-    for start in range(0, total, SUB):
-        look_up_weight(0, start)
+            weight_table[t * width : (t + 1) * width, z * LANES : (z + 1) * LANES] = jnp.concatenate(both, 0).astype(BF)
+    loop(0, total, functools.partial(build_onehot, 0), 1)
+    arrivals0 = weigh(0)
 
     pltpu.make_async_copy(raw, raw, local_sem.at[6]).wait()
     for r in range(0, width, 2):
@@ -347,17 +352,6 @@
         for i in range(2):
             phi[pl.ds(r + i, blocks, stride=width), :] = ordered[:, i * LANES : (i + 1) * LANES]
 
-    for copy in cell_copies:
-        copy.wait_recv()
-    cell = cell1[...]
-    high_rows[...] = (cell >> 8).astype(F32)
-    low_rows[...] = (cell & (LOW - 1)).astype(F32)
-    for start in range(0, total, SUB):
-        build_onehot(1, start)
-    arrivals1 = deposit_count(1)
-    for start in range(0, total, SUB):
-        look_up_weight(1, start)
-
     load_react.wait()
     react_t = react[...].T
     r_high = react_t.astype(BF).astype(F32)
@@ -366,7 +360,7 @@
 
     def advance(step, piece, start):
         cut = pl.ds(start, SUB)
-        value = look_up(step, start)
+        value = look_up(step, start, table)
         w8 = weight[step, :, cut]
         mixed = piece + jnp.concatenate([w8, w8], 0) * (value - piece)
         upper = mixed.astype(BF)
@@ -374,6 +368,11 @@
         stack = jnp.concatenate([upper, lower, upper], 0)
         return mixed + REACT_STEP * jnp.tanh(jnp.dot(react3, stack, preferred_element_type=F32))
 
+    def piece0(index):
+        base = pl.multiple_of(index * (rows_of * width), rows_of * width)
+        rows = phi[pl.ds(base, rows_of * width), :]
+        return jnp.concatenate([rows[r * width : (r + 1) * width] for r in range(rows_of)], 1)
+
     def deposit(step, rows, start):
         cut = pl.ds(start, SUB)
         at = high[step, :, cut]
@@ -381,9 +380,9 @@
         spread = jnp.concatenate([jnp.where(at == t, r, 0.0) for r in rows for t in range(TILES)], 0).astype(BF)
         return lax.dot_general(spread, onehot[step, :, cut], NT, preferred_element_type=F32)
 
-    def set_moment(kind, sums):
-        moment[kind, 0] = sums[:, :LANES]
-        moment[kind, 1] = sums[:, LANES:]
+    def add_moment(kind, sums):
+        moment[kind, 0] += sums[:, :LANES]
+        moment[kind, 1] += sums[:, LANES:]
 
     def owner_rows(kind, owner, z):
         return jnp.concatenate(
@@ -396,24 +395,28 @@
     for copy in copies:
         copy.wait_recv()
     build_table(0)
-    sums = jnp.zeros((TILES * width, LOW), F32)
+    moment[0] = jnp.zeros((2, TILES * width, LANES), F32)
     moves = []
-    for start in list(range(half, total, SUB)) + list(range(0, half, SUB)):
-        first = start // LANES
-        piece = jnp.concatenate([phi[r * width : (r + 1) * width, :] for r in range(first, first + rows_of)], 1)
-        stepped = advance(0, piece, start)
-        if start < half:
-            moved[:, start : start + SUB] = stepped
-        else:
-            side, at = (start - half) // part, (start - half) % part
-            mig_send[side, :, at : at + SUB] = stepped.astype(BF)
-            if at + SUB == part:
-                where = (g, down) if side == 0 else (g, up)
-                moves.append(
-                    send(mig_send.at[side], mig_got.at[1 - side], mig_ssem.at[side], mig_rsem.at[1 - side], where)
-                )
-        sums = sums + deposit(0, [stepped], start)
-    set_moment(0, sums)
+    for side in range(2):
+        begin = half + side * part
+
+        def leaving(index, start):
+            stepped = advance(0, piece0(index), start)
+            mig_send[side, :, pl.ds(pl.multiple_of(start - begin, SUB), SUB)] = stepped.astype(BF)
+            add_moment(0, deposit(0, [stepped], start))
+
+        loop(begin, begin + part, leaving, 4)
+        where = (g, down) if side == 0 else (g, up)
+        moves.append(
+            send(mig_send.at[side], mig_got.at[1 - side], mig_ssem.at[side], mig_rsem.at[1 - side], where)
+        )
+
+    def staying(index, start):
+        stepped = advance(0, piece0(index), start)
+        moved[:, pl.ds(start, SUB)] = stepped
+        add_moment(0, deposit(0, [stepped], start))
+
+    loop(0, half, staying, 4)
     for owner in range(n_grp):
         for z in range(2):
             sum_send0[owner, z] = owner_rows(0, owner, z)
@@ -424,36 +427,41 @@
     diffused = diffuse_own(0, current)
     count = total_count(0, arrivals0)
     first = [sum_send0[g, z].astype(F32) for z in range(2)]
+    for copy in cell_copies:
+        copy.wait_recv()
+    cell = cell1[...]
+    high_rows[...] = (cell >> 8).astype(F32)
+    low_rows[...] = (cell & (LOW - 1)).astype(F32)
+    loop(0, total, functools.partial(build_onehot, 1), 1)
     for copy in sum_copies:
         copy.wait_recv()
     for i in range(n_grp - 1):
         first = [first[z] + sum_got0[i, z].astype(F32) for z in range(2)]
     current = refresh(diffused, first, count)
     copies = exchange(1, current)
-    count = total_count(1, arrivals1)
+    arrivals1 = weigh(1)
+    moment[...] = jnp.zeros((2, 2, TILES * width, LANES), F32)
     for copy in moves:
         copy.wait_recv()
+    for side in range(2):
+        moved[:, half + side * part : half + (side + 1) * part] = mig_got[side].astype(F32)
     for copy in copies:
         copy.wait_recv()
     build_table(1)
 
-    sums = jnp.zeros((2 * TILES * width, LOW), F32)
-    for start in range(0, total, SUB):
+    def second_step(_, start):
         cut = pl.ds(start, SUB)
-        if start < half:
-            piece = moved[:, cut]
-        else:
-            side, at = (start - half) // part, (start - half) % part
-            piece = mig_got[side, :, at : at + SUB].astype(F32)
-        stepped = advance(1, piece, start)
+        stepped = advance(1, moved[:, cut], start)
         dead = high[1, :, cut] < 0
         kept = jnp.where(jnp.concatenate([dead, dead], 0), 0.0, stepped)
         particles_new[:, cut] = kept
-        sums = sums + deposit(1, [kept, kept * stepped], start)
+        sums = deposit(1, [kept, kept * stepped], start)
+        add_moment(0, sums[: TILES * width])
+        add_moment(1, sums[TILES * width :])
+
+    loop(0, total, second_step, 4)
     store_particles = pltpu.make_async_copy(particles_new, particles_out, local_sem.at[0])
     store_particles.start()
-    set_moment(0, sums[: TILES * width])
-    set_moment(1, sums[TILES * width :])
     for owner in range(n_grp):
         for kind in range(2):
             for z in range(2):
@@ -463,6 +471,7 @@
         for i in range(n_grp - 1)
     ]
     diffused = diffuse_own(1, current)
+    count = total_count(1, arrivals1)
     first = [sum_send1[g, 0, z].astype(F32) for z in range(2)]
     second = [sum_send1[g, 1, z].astype(F32) for z in range(2)]
     for copy in sum_copies:
@@ -543,7 +552,7 @@
                 pltpu.VMEM((blocks, LANES), I32),
                 pltpu.VMEM((blocks, LANES), I32),
                 pltpu.VMEM((blocks * width, LANES), F32),
-                pltpu.VMEM((width, total // 2), F32),
+                pltpu.VMEM((width, total), F32),
                 pltpu.VMEM((2, TILES, total), I32),
                 pltpu.VMEM((2, 8, total), F32),
                 pltpu.VMEM((2, LOW, total), BF),
@@ -554,6 +563,7 @@
                 pltpu.VMEM((2, 2, tile, LANES), BF),
                 pltpu.VMEM((2, 4, rows, LANES), BF),
                 pltpu.VMEM((2, rows, LANES), F32),
+                pltpu.VMEM((rows, LOW), BF),
                 pltpu.VMEM((rows, LOW), BF),
                 pltpu.VMEM((2, 2, rows, LANES), F32),
                 pltpu.VMEM((n_grp, 2, tile, LANES), BF),

time: 49.1 us -> 46.1 us (0.939)
  Pallas kernels: 48.3 us -> 45.2 us
    pallas_call x1, Pallas kernels: 46.5 us -> 43.4 us  [shards(): pl.pallas_call(functools.partial(kernel, n_grp, n_sp), out_shape=shapes,...]
where the time goes in v3:
time: 46.1 us; the launch traced here: 45.9 us
  Pallas kernels  45.2 us (98%)
  between operations  0.64 us (1%)
    pallas_call x1, Pallas kernels, shards(): pl.pallas_call(functools.partial(kernel, n_grp, n_sp), out_shape=shapes,...  43.4 us
    pallas_call x1, Pallas kernels, shards(): pl.pallas_call(put_out, out_shape=(shapes[2], shapes[0], shapes[1]), in_s...  1.86 us

profile of v3, /device:TPU:1, one launch (start us, length us, event | category | flops | bytes accessed | tf_op | source)
XLA Modules:
  0.0 45.9 jit_solution(7050386213105319596)
XLA Ops:
  0.6 43.4 %mixing.1 = (f32[2,2,1024]{2,1,0:T(2,128)}, f32[2,2,1024]{2,1,0:T(2,128)}, f32[16,8192]{1,0:T(8,128)}) custom-call(f32[2,2,1024]{2,1,0:T(2,128)} %field_hbm.1, f32[2,1024]{1,0:T(2,128)} %rate_hbm.1, f32[16,16]{1,0:T(8,128)} %react_hbm.1, f32[16,8192]{1,0:T(8,128)} %particles.1, s32[2,8192]{1,0:T(2,128)} %cells.1, s32[64]{0:T(128)} %counts_hbm.1, s32[64]{0:T(128)} %dest_hbm.1), custom_call_target="tpu_custom_call" | custom-call | tf_op jit(solution)/shard_map/mixing/pallas_call | solution.py:536
  44.0 1.9 %put_out.1 = (f32[16,8192]{1,0:T(8,128)}, f32[2,2,1024]{2,1,0:T(2,128)}, f32[2,2,1024]{2,1,0:T(2,128)}) custom-call(f32[16,8192]{1,0:T(8,128)} %get-tuple-element.9.particles, f32[2,2,1024]{2,1,0:T(2,128)} %get-tuple-element.10.field, f32[2,2,1024]{2,1,0:T(2,128)} %get-tuple-element.11.spread), custom_call_target="tpu_custom_call" | custom-call | tf_op jit(solution)/shard_map/put_out/pallas_call | solution.py:595

commit v4 on v3

--- a/solution.py
+++ b/solution.py
@@ -68,9 +68,6 @@
     high,
     weight,
     onehot,
-    particles_new,
-    field_new,
-    spread_new,
     own_planes,
     plane_send,
     planes,
@@ -112,12 +109,17 @@
     down = lax.rem(s + n_sp - 1, n_sp)
     mine = pl.ds(pl.multiple_of(g * tile, tile), tile)
 
-    def peer(d):
-        return lax.rem(g + d, n_grp)
-
-    others = [(peer(d), s) for d in range(1, n_grp)]
-    above = [(peer(d), up) for d in range(n_grp)]
-    below = [(peer(d), down) for d in range(n_grp)]
+    across = n_grp // 2
+    row, column = g // across, lax.rem(g, across)
+
+    def peer(dy, dx):
+        return lax.rem(row + dy, 2) * across + lax.rem(column + dx, across)
+
+    turns = sorted(range(across), key=lambda dx: -min(dx, across - dx))
+    ranked = [peer(dy, dx) for dy in (1, 0) for dx in turns]
+    others = [(p, s) for p in ranked[:-1]]
+    above = [(p, up) for p in ranked]
+    below = [(p, down) for p in ranked]
     barrier = pltpu.get_barrier_semaphore()
     for where in others + above + below:
         pl.semaphore_signal(barrier, inc=1, device_id=where, device_id_type=MESH)
@@ -433,13 +435,13 @@
     high_rows[...] = (cell >> 8).astype(F32)
     low_rows[...] = (cell & (LOW - 1)).astype(F32)
     loop(0, total, functools.partial(build_onehot, 1), 1)
+    arrivals1 = weigh(1)
     for copy in sum_copies:
         copy.wait_recv()
     for i in range(n_grp - 1):
         first = [first[z] + sum_got0[i, z].astype(F32) for z in range(2)]
     current = refresh(diffused, first, count)
     copies = exchange(1, current)
-    arrivals1 = weigh(1)
     moment[...] = jnp.zeros((2, 2, TILES * width, LANES), F32)
     for copy in moves:
         copy.wait_recv()
@@ -454,14 +456,12 @@
         stepped = advance(1, moved[:, cut], start)
         dead = high[1, :, cut] < 0
         kept = jnp.where(jnp.concatenate([dead, dead], 0), 0.0, stepped)
-        particles_new[:, cut] = kept
+        particles_out[:, cut] = kept
         sums = deposit(1, [kept, kept * stepped], start)
         add_moment(0, sums[: TILES * width])
         add_moment(1, sums[TILES * width :])
 
     loop(0, total, second_step, 4)
-    store_particles = pltpu.make_async_copy(particles_new, particles_out, local_sem.at[0])
-    store_particles.start()
     for owner in range(n_grp):
         for kind in range(2):
             for z in range(2):
@@ -486,32 +486,21 @@
         for j in range(own):
             for t in range(TILES):
                 row, cut = j * TILES + t, slice(t * LANES, (t + 1) * LANES)
-                field_new[j, z : z + 1, cut] = refreshed[z][row : row + 1, :]
-                spread_new[j, z : z + 1, cut] = spread[row : row + 1, :]
-    store_field = pltpu.make_async_copy(field_new, field_out, local_sem.at[1])
-    store_spread = pltpu.make_async_copy(spread_new, spread_out, local_sem.at[2])
-    store_field.start()
-    store_spread.start()
+                field_out[j, z : z + 1, cut] = refreshed[z][row : row + 1, :]
+                spread_out[j, z : z + 1, cut] = spread[row : row + 1, :]
     for copy in pending:
         copy.wait_send()
-    for copy in (store_particles, store_field, store_spread):
+
+
+def put_out(particles, field, spread, particles_out, field_out, spread_out, sem):
+    copies = [
+        pltpu.make_async_copy(src, dst, sem.at[i])
+        for i, (src, dst) in enumerate([(particles, particles_out), (field, field_out), (spread, spread_out)])
+    ]
+    for copy in copies:
+        copy.start()
+    for copy in copies:
         copy.wait()
-
-
-def put_out(particles, field, spread, particles_out, field_out, spread_out, *scratch):
-    buffers, sem = scratch[:-1], scratch[-1]
-    ways = []
-    for i, (src, dst) in enumerate([(particles, particles_out), (field, field_out), (spread, spread_out)]):
-        take = pltpu.make_async_copy(src, buffers[i], sem.at[i])
-        put = pltpu.make_async_copy(buffers[i], dst, sem.at[i])
-        ways.append((take, put))
-    for take, _ in ways:
-        take.start()
-    for take, put in ways:
-        take.wait()
-        put.start()
-    for _, put in ways:
-        put.wait()
 
 
 def solution(mesh):
@@ -524,6 +513,7 @@
         part = total // 4
         tile = own * TILES
         rows = width * TILES
+        vmem = pl.BlockSpec(memory_space=pltpu.VMEM)
         hbm = pl.BlockSpec(memory_space=pltpu.HBM)
         others = n_grp - 1
         spread = 3 * n_grp - 1
@@ -533,11 +523,15 @@
             jax.ShapeDtypeStruct(field.shape, F32),
             jax.ShapeDtypeStruct(particles.shape, F32),
         )
+        field, mix_rate, react, particles, cells, counts, dest = [
+            pltpu.with_memory_space_constraint(a, pltpu.HBM)
+            for a in (field, mix_rate, react, particles, cells, counts, dest)
+        ]
         results = pl.pallas_call(
             functools.partial(kernel, n_grp, n_sp),
             out_shape=shapes,
             in_specs=[hbm] * 7,
-            out_specs=(hbm, hbm, hbm),
+            out_specs=(vmem, vmem, vmem),
             scratch_shapes=[
                 pltpu.VMEM(field.shape, F32),
                 pltpu.VMEM(mix_rate.shape, F32),
@@ -556,9 +550,6 @@
                 pltpu.VMEM((2, TILES, total), I32),
                 pltpu.VMEM((2, 8, total), F32),
                 pltpu.VMEM((2, LOW, total), BF),
-                pltpu.VMEM(particles.shape, F32),
-                pltpu.VMEM(field.shape, F32),
-                pltpu.VMEM(field.shape, F32),
                 pltpu.VMEM((2, tile, LANES), F32),
                 pltpu.VMEM((2, 2, tile, LANES), BF),
                 pltpu.VMEM((2, 4, rows, LANES), BF),
@@ -587,7 +578,7 @@
                 dma((2, others)),
             ],
             compiler_params=pltpu.CompilerParams(
-                collective_id=0, has_side_effects=True, vmem_limit_bytes=67043328
+                collective_id=0, has_side_effects=True, vmem_limit_bytes=50331648
             ),
             name="mixing",
         )(field, mix_rate, react, particles, cells, counts, dest)
@@ -595,15 +586,10 @@
         particles_new, field_new, spread_new = pl.pallas_call(
             put_out,
             out_shape=(shapes[2], shapes[0], shapes[1]),
-            in_specs=[hbm] * 3,
+            in_specs=[vmem] * 3,
             out_specs=(hbm, hbm, hbm),
-            scratch_shapes=[
-                pltpu.VMEM(particles.shape, F32),
-                pltpu.VMEM(field.shape, F32),
-                pltpu.VMEM(field.shape, F32),
-                dma((3,)),
-            ],
-            compiler_params=pltpu.CompilerParams(vmem_limit_bytes=67043328),
+            scratch_shapes=[dma((3,))],
+            compiler_params=pltpu.CompilerParams(vmem_limit_bytes=4194304),
             name="put_out",
         )(particles_new, field_new, spread_new)
         return field_new, spread_new, particles_new

time: 46.1 us -> 43.9 us (0.952)
  Pallas kernels: 45.2 us -> 43.1 us
    pallas_call x1, Pallas kernels: 43.4 us -> 42.2 us  [shards(): pl.pallas_call(functools.partial(kernel, n_grp, n_sp), out_shape=shapes,...]
    pallas_call x1, Pallas kernels: 1.86 us -> 0.83 us  [shards(): pl.pallas_call(put_out, out_shape=(shapes[2], shapes[0], shapes[1]), in_s...]
where the time goes in v4:
time: 43.9 us; the launch traced here: 43.7 us
  Pallas kernels  43.1 us (98%)
  between operations  0.64 us (1%)
    pallas_call x1, Pallas kernels, shards(): pl.pallas_call(functools.partial(kernel, n_grp, n_sp), out_shape=shapes,...  42.2 us

profile of v4, /device:TPU:1, one launch (start us, length us, event | category | flops | bytes accessed | tf_op | source)
XLA Modules:
  0.0 43.7 jit_solution(11632164484640162768)
XLA Ops:
  0.6 42.2 %mixing.1 = (f32[2,2,1024]{2,1,0:T(2,128)S(1)}, f32[2,2,1024]{2,1,0:T(2,128)S(1)}, f32[16,8192]{1,0:T(8,128)S(1)}) custom-call(f32[2,2,1024]{2,1,0:T(2,128)} %field_hbm.1, f32[2,1024]{1,0:T(2,128)} %rate_hbm.1, f32[16,16]{1,0:T(8,128)} %react_hbm.1, f32[16,8192]{1,0:T(8,128)} %particles.1, s32[2,8192]{1,0:T(2,128)} %cells.1, s32[64]{0:T(128)} %counts_hbm.1, ...), custom_call_target="tpu_custom_call" | custom-call | tf_op jit(solution)/shard_map/mixing/pallas_call | solution.py:530
  42.9 0.8 %put_out.1 = (f32[16,8192]{1,0:T(8,128)}, f32[2,2,1024]{2,1,0:T(2,128)}, f32[2,2,1024]{2,1,0:T(2,128)}) custom-call(f32[16,8192]{1,0:T(8,128)S(1)} %get-tuple-element.9.particles, f32[2,2,1024]{2,1,0:T(2,128)S(1)} %get-tuple-element.10.field, f32[2,2,1024]{2,1,0:T(2,128)S(1)} %get-tuple-element.11.spread), custom_call_target="tpu_custom_call" | custom-call | tf_op jit(solution)/shard_map/put_out/pallas_call | solution.py:586

commit v5 on v4

--- a/solution.py
+++ b/solution.py
@@ -296,7 +296,7 @@
             both = look_up(step, start, weight_table)
             weight[step, :, cut] = both[:8] + both[8:]
 
-        loop(0, total, add, 1)
+        loop(0, total, add, 2)
         return [
             send(
                 count_own.at[step],
@@ -340,7 +340,7 @@
             cut = slice(t * LANES, (t + 1) * LANES)
             both = [jnp.broadcast_to(w[z : z + 1, cut], (8, LANES)) for w in (w_high, w_low)]
             weight_table[t * width : (t + 1) * width, z * LANES : (z + 1) * LANES] = jnp.concatenate(both, 0).astype(BF)
-    loop(0, total, functools.partial(build_onehot, 0), 1)
+    loop(0, total, functools.partial(build_onehot, 0), 2)
     arrivals0 = weigh(0)
 
     pltpu.make_async_copy(raw, raw, local_sem.at[6]).wait()

time: 43.9 us -> 43.9 us (level)
  no operation moved by 1% of the time
where the time goes in v5:
time: 43.9 us; the launch traced here: 43.7 us
  Pallas kernels  43.1 us (98%)
  between operations  0.64 us (1%)
    pallas_call x1, Pallas kernels, shards(): pl.pallas_call(functools.partial(kernel, n_grp, n_sp), out_shape=shapes,...  42.3 us

profile of v5, /device:TPU:1, one launch (start us, length us, event | category | flops | bytes accessed | tf_op | source)
XLA Modules:
  0.0 43.7 jit_solution(11536574426744981957)
XLA Ops:
  0.6 42.3 %mixing.1 = (f32[2,2,1024]{2,1,0:T(2,128)S(1)}, f32[2,2,1024]{2,1,0:T(2,128)S(1)}, f32[16,8192]{1,0:T(8,128)S(1)}) custom-call(f32[2,2,1024]{2,1,0:T(2,128)} %field_hbm.1, f32[2,1024]{1,0:T(2,128)} %rate_hbm.1, f32[16,16]{1,0:T(8,128)} %react_hbm.1, f32[16,8192]{1,0:T(8,128)} %particles.1, s32[2,8192]{1,0:T(2,128)} %cells.1, s32[64]{0:T(128)} %counts_hbm.1, ...), custom_call_target="tpu_custom_call" | custom-call | tf_op jit(solution)/shard_map/mixing/pallas_call | solution.py:530
  42.9 0.8 %put_out.1 = (f32[16,8192]{1,0:T(8,128)}, f32[2,2,1024]{2,1,0:T(2,128)}, f32[2,2,1024]{2,1,0:T(2,128)}) custom-call(f32[16,8192]{1,0:T(8,128)S(1)} %get-tuple-element.9.particles, f32[2,2,1024]{2,1,0:T(2,128)S(1)} %get-tuple-element.10.field, f32[2,2,1024]{2,1,0:T(2,128)S(1)} %get-tuple-element.11.spread), custom_call_target="tpu_custom_call" | custom-call | tf_op jit(solution)/shard_map/put_out/pallas_call | solution.py:586
